TPU v7x, 32 devices: a whole 2x2x4 slice. The times are simulated.
32 devices in a mesh: groups: 2 (over x), rows: 16 (over z, y, core).
Axes of the slice: x: 2, y: 2, z: 4, core: 2. Of those that a mesh axis runs over, the one named last changes fastest.
Arguments:
- phase: float32 [512, 2048], P(('groups', 'rows')), parts along dimension 0, may hold values from -3.140625 to 3.140625
Outputs:
- filtered: float32 [2, 512, 2048], P(None, ('groups', 'rows')), parts along dimension 1
- profile: float32 [6, 16], P('groups'), parts along dimension 0
There are 2 independent parts, one for each index of `groups`. A program takes and returns all parts, laid end to end along the dimension named above; each array names one. Nothing has to cross between parts.
All inputs are finite; a program needn't handle non-finite values.
Results may differ from a plain program's by a relative error of at most 0.00012.
Values sent between devices are 32-bit elements; how exact they have to be, the bound alone decides.
No kernel may reach another device: no remote copies, remote signals or barrier semaphores. Data moves between devices by JAX's collectives and lax.ppermute only.
A program may use at most 64 MiB of HBM per device.

v0:
```python
import functools
import math

import jax
import jax.numpy as jnp
from jax import lax
from jax.experimental import pallas as pl
from jax.experimental.pallas import tpu as pltpu
from jax.sharding import PartitionSpec as P

ITERS = 3
EPS = 1e-06
LANES = 128
HALO = 3

SIN = (1.000000000e+00, -1.666666662e-01, 8.333330977e-03, -1.984086143e-04, 2.752528078e-06, -2.388938418e-08)
COS = (9.999999998e-01, -4.999999936e-01, 4.166663620e-02, -1.388836069e-03, 2.476012736e-05, -2.605092951e-07)


def rotated(value, k, size, sign):
    re, im = value
    half = math.sqrt(0.5)
    if k == 0:
        return re, im
    if 4 * k == size:
        return (im, -re) if sign < 0 else (-im, re)
    if 8 * k == size:
        return ((re + im) * half, (im - re) * half) if sign < 0 else ((re - im) * half, (im + re) * half)
    if 8 * k == 3 * size:
        return ((im - re) * half, (re + im) * -half) if sign < 0 else ((re + im) * -half, (re - im) * half)
    c = math.cos(2 * math.pi * k / size)
    s = sign * math.sin(2 * math.pi * k / size)
    return re * c - im * s, im * c + re * s


def plus(a, b):
    return a[0] + b[0], a[1] + b[1]


def minus(a, b):
    return a[0] - b[0], a[1] - b[1]


def fft(values, sign):
    size = len(values)
    if size == 1:
        return values
    even = fft(values[0::2], sign)
    odd = fft(values[1::2], sign)
    turned = [rotated(odd[k], k, size, sign) for k in range(size // 2)]
    return [plus(e, o) for e, o in zip(even, turned)] + [minus(e, o) for e, o in zip(even, turned)]


def polynomial(coefficients, w):
    result = jnp.full_like(w, coefficients[-1])
    for c in coefficients[-2::-1]:
        result = result * w + c
    return result


def cos_sin(x):
    u = (jnp.abs(x) - jnp.float32(math.pi / 2)) + jnp.float32(4.371139e-08)
    w = u * u
    cosine = -(u * polynomial(SIN, w))
    sine = polynomial(COS, w)
    return cosine, jnp.where(x < 0, -sine, sine)


def swap_bits(values, lane):
    values = list(values)
    bit = 1
    while bit < len(values):
        clear = (lane & bit) == 0
        for p in range(len(values)):
            if p & bit == 0:
                low, high = values[p], values[p | bit]
                values[p] = jnp.where(clear, low, pltpu.roll(high, bit, 1))
                values[p | bit] = jnp.where(clear, pltpu.roll(low, LANES - bit, 1), high)
        bit *= 2
    return values


def ramp(t):
    return 1.0 - abs(t - 15.5) / 16.0


def filter_kernel(slabs, blocks, tiles, packed, in_ref, out_ref, zr, zi, yr, yi, wr, wi, gain):
    tile = lax.axis_index("rows")
    per_tile = LANES // slabs
    lane = lax.broadcasted_iota(jnp.int32, (8, LANES), 1)
    sub = lax.broadcasted_iota(jnp.int32, (8, LANES), 0)
    slab = lane % slabs
    not_last = slab != slabs - 1
    not_first = slab != 0
    place = lane // slabs

    def inside(h, step):
        position = (h * per_tile + place + step) % (tiles * per_tile)
        relative = jnp.where(position < blocks + HALO, position, position - tiles * per_tile)
        column = tile * blocks + relative
        return jnp.where((column >= 0) & (column < slabs * blocks), 1.0, 0.0)

    here = [inside(h, 0) for h in range(tiles)]
    both = [here[h] * inside(h, 1) for h in range(tiles)]

    def right(values):
        if per_tile == 1:
            return [values[(h + 1) % tiles] for h in range(tiles)]
        moved = [pltpu.roll(v, LANES - slabs, 1) for v in values]
        return [jnp.where(lane < LANES - slabs, moved[h], moved[(h + 1) % tiles]) for h in range(tiles)]

    def left(values):
        if per_tile == 1:
            return [values[h - 1] for h in range(tiles)]
        moved = [pltpu.roll(v, slabs, 1) for v in values]
        return [jnp.where(lane < slabs, moved[h - 1], moved[h]) for h in range(tiles)]

    def below(value):
        return jnp.where(not_last, pltpu.roll(value, LANES - 1, 1), 0.0)

    def above(value):
        return jnp.where(not_first, pltpu.roll(value, 1, 1), 0.0)

    for h in range(tiles):
        for g in range(2):
            if packed:
                phases = swap_bits([in_ref[a, h * 16 + g * 8 : h * 16 + g * 8 + 8, :] for a in range(16)], lane)
            else:
                phases = [in_ref[h, s, g * 8 : g * 8 + 8, :] for s in range(16)]
            for s in range(16):
                cosine, sine = cos_sin(phases[s])
                zr[h * 16 + s, g * 8 : g * 8 + 8, :] = cosine * here[h]
                zi[h * 16 + s, g * 8 : g * 8 + 8, :] = sine * here[h]

    def measure_z():
        total = jnp.zeros((8, LANES), jnp.float32)
        energy = [jnp.zeros((8, LANES), jnp.float32) for _ in range(tiles)]
        for h in range(1, tiles):
            for s in range(16):
                for g in range(2):
                    re = zr[h * 16 + s, g * 8 : g * 8 + 8, :]
                    im = zi[h * 16 + s, g * 8 : g * 8 + 8, :]
                    energy[h] = energy[h] + (re * re + im * im)

        def column(s, shifted):
            halves = []
            for ref in (zr, zi):
                top = ref[s, 0:8, :]
                low = ref[s, 8:16, :]
                if shifted:
                    top = right([ref[h * 16, 0:8, :] for h in range(tiles)])[0]
                    low = right([ref[h * 16, 8:16, :] for h in range(tiles)])[0]
                turned = [pltpu.roll(v, 7, 0) for v in (top, low, below(top))]
                halves.append((top, low, jnp.where(sub < 7, turned[0], turned[1]), jnp.where(sub < 7, turned[1], turned[2])))
            (r0, r1, r0d, r1d), (i0, i1, i0d, i1d) = halves
            vertical = (i0 * r0d - r0 * i0d, i1 * r1d - r1 * i1d)
            return (r0, i0, r0d, i0d), (r1, i1, r1d, i1d), vertical

        current = column(0, False)
        for s in range(16):
            following = column(s + 1, False) if s < 15 else column(0, True)
            for g in range(2):
                r, i, rd, idn = current[g]
                rn, in_, rdn, idnn = following[g]
                energy[0] = energy[0] + (r * r + i * i)
                across = i * rn - r * in_
                across_down = idn * rdn - rd * idnn
                loop = (across - across_down) + (following[2][g] - current[2][g])
                total = total + loop * loop
            current = following
        summed = [jnp.broadcast_to(jnp.sum(e, axis=0, keepdims=True), (8, LANES)) for e in energy]
        tall = [e + below(e) for e in summed]
        wide = right(tall)
        for h in range(tiles):
            gain[h * 8 : h * 8 + 8, :] = 1.0 / ((tall[h] + wide[h]) + EPS)
        return jnp.sum(total)

    def forward_columns(g):
        rows = pl.ds(pl.multiple_of(g * 8, 8), 8)
        first = [[None] * 16 for _ in range(tiles)]
        second = [[None] * 16 for _ in range(tiles)]
        for s in range(16):
            re = [zr[h * 16 + s, rows, :] for h in range(tiles)]
            im = [zi[h * 16 + s, rows, :] for h in range(tiles)]
            for h, (a, b) in enumerate(zip(right(re), right(im))):
                first[h][s] = (re[h], im[h])
                second[h][s] = (a, b)
        for h in range(tiles):
            sums = [plus(a, b) for a, b in zip(first[h], second[h])]
            differences = [rotated(minus(a, b), s, 32, -1) for s, (a, b) in enumerate(zip(first[h], second[h]))]
            for parity, half in enumerate((sums, differences)):
                for m, (re, im) in enumerate(fft(half, -1)):
                    at = pl.ds((h * 32 + 2 * m + parity) * 17 + g * 8, 8)
                    yr[at, :] = re
                    yi[at, :] = im

    def windows(unit):
        h = unit // 4
        q = unit % 4
        base = (h * 32 + q * 8) * 17
        scale = gain[pl.ds(pl.multiple_of(h * 8, 8), 8), :]
        first = []
        second = []
        for t in range(16):
            at = pl.ds(base + t, 8, stride=17)
            re = yr[at, :]
            im = yi[at, :]
            first.append((re, im))
            second.append((below(re), below(im)))
        sums = [plus(a, b) for a, b in zip(first, second)]
        differences = [rotated(minus(a, b), t, 32, -1) for t, (a, b) in enumerate(zip(first, second))]
        back = []
        for half in (sums, differences):
            filtered = []
            for re, im in fft(half, -1):
                power = (re * re + im * im) * scale
                factor = lax.rsqrt(lax.rsqrt(power))
                filtered.append((re * factor, im * factor))
            back.append(fft(filtered, 1))
        for t in range(16):
            even = back[0][t]
            odd = rotated(back[1][t], t, 32, 1)
            upper = plus(even, odd)
            lower = minus(even, odd)
            at = pl.ds((h * 16 + t) * 33 + q * 8, 8)
            wr[at, :] = upper[0] * (ramp(t) / 32) + above(lower[0] * (ramp(t + 16) / 32))
            wi[at, :] = upper[1] * (ramp(t) / 32) + above(lower[1] * (ramp(t + 16) / 32))

    def inverse_columns(g):
        rows = pl.ds(pl.multiple_of(g * 8, 8), 8)
        kept = []
        passed = []
        for h in range(tiles):
            back = []
            for parity in range(2):
                values = []
                for m in range(16):
                    at = pl.ds((h * 16 + g * 8) * 33 + 2 * m + parity, 8, stride=33)
                    values.append((wr[at, :], wi[at, :]))
                back.append(fft(values, 1))
            own = []
            other = []
            for s in range(16):
                odd = rotated(back[1][s], s, 32, 1)
                near = here[h] * (ramp(s) / 32)
                far = both[h] * (ramp(s + 16) / 32)
                a = plus(back[0][s], odd)
                b = minus(back[0][s], odd)
                own.append((a[0] * near, a[1] * near))
                other.append((b[0] * far, b[1] * far))
            kept.append(own)
            passed.append(other)
        for s in range(16):
            for part, ref in enumerate((zr, zi)):
                arrived = left([passed[h][s][part] for h in range(tiles)])
                for h in range(tiles):
                    ref[h * 16 + s, rows, :] = kept[h][s][part] + arrived[h]

    def run(count, body):
        lax.fori_loop(0, count, lambda i, c: (body(i), c)[1], 0)

    def iteration(step, carry):
        total = measure_z()
        out_ref_row(step, total)
        run(2, forward_columns)
        run(4 * tiles, windows)
        run(2, inverse_columns)
        return carry

    if packed:

        def out_ref_row(step, total):
            for a in range(16):
                out_ref[a, pl.ds(32 + step, 1), :] = jnp.full((1, LANES), total)

    else:

        def out_ref_row(step, total):
            out_ref[32, pl.ds(step, 1), :] = jnp.full((1, LANES), total)

    lax.fori_loop(0, ITERS, iteration, 0)

    for part, ref in enumerate((zr, zi)):
        for g in range(2):
            values = [ref[s, g * 8 : g * 8 + 8, :] for s in range(16)]
            if packed:
                for a, value in enumerate(swap_bits(values, lane)):
                    out_ref[a, part * 16 + g * 8 : part * 16 + g * 8 + 8, :] = value
            else:
                for s, value in enumerate(values):
                    out_ref[part * 16 + s, g * 8 : g * 8 + 8, :] = value


def filter_tiles(slabs, blocks, tiles, packed, data):
    shape = (16, 40, LANES) if packed else (33, 16, LANES)
    body = functools.partial(filter_kernel, slabs, blocks, tiles, packed)
    return pl.pallas_call(
        body,
        out_shape=jax.ShapeDtypeStruct(shape, jnp.float32),
        in_specs=[pl.BlockSpec(memory_space=pltpu.VMEM)],
        out_specs=pl.BlockSpec(memory_space=pltpu.VMEM),
        scratch_shapes=[pltpu.VMEM((tiles * 16, 16, LANES), jnp.float32)] * 2
        + [pltpu.VMEM((tiles * 32 * 17 + 8, LANES), jnp.float32)] * 2
        + [pltpu.VMEM((tiles * 16 * 33 + 8, LANES), jnp.float32)] * 2
        + [pltpu.VMEM((tiles * 8, LANES), jnp.float32)],
        name="filter_tiles",
    )(data)


def ring_of_blocks(phase, devices, blocks, tiles):
    per_tile = LANES // devices
    ring = tiles * per_tile
    width = phase.shape[1]
    padded = jnp.pad(phase, ((0, 0), (HALO * 16, (ring + HALO) * 16)))
    pieces = []
    for d in range(devices):
        start = d * blocks * 16
        ahead = padded[:, start + HALO * 16 : start + (blocks + 2 * HALO) * 16]
        behind = padded[:, start : start + HALO * 16]
        gap = jnp.zeros((16, (ring - blocks - 2 * HALO) * 16), phase.dtype)
        pieces.append(jnp.concatenate([ahead, gap, behind], axis=1))
    return jnp.stack(pieces)


def per_device(phase):
    devices = lax.axis_size("rows")
    height, width = phase.shape
    blocks = width // (16 * devices)
    per_tile = LANES // devices
    if height != 16 or LANES % devices or blocks * 16 * devices != width or blocks != per_tile:
        raise ValueError("unsupported sizes")
    scale = 1.0 / (height * devices * 128.0)
    if devices == 16:
        tiles = 2
        columns = phase.reshape(16, devices, LANES).transpose(1, 0, 2)
        empty = jnp.zeros((1, 16, LANES), phase.dtype)
        after = jnp.concatenate([columns[1:], empty])
        before = jnp.concatenate([empty, columns[:-1]])
        lane = lax.broadcasted_iota(jnp.int32, columns.shape, 2)
        data = jnp.concatenate([columns, jnp.where(lane < LANES // 2, after, before)], axis=1)
        data = lax.all_to_all(data, "rows", 0, 0)
        result = filter_tiles(devices, blocks, tiles, True, data)
        result = lax.all_to_all(result, "rows", 0, 0)
        field = result[:, :32].reshape(devices, 2, 16, LANES).transpose(1, 2, 0, 3).reshape(2, 16, width)
        profile = result[:, 32 : 32 + ITERS, 0].T
        return field, profile * scale
    tiles = -(-(blocks + 2 * HALO) // per_tile)
    data = lax.all_to_all(ring_of_blocks(phase, devices, blocks, tiles), "rows", 0, 0)
    data = data.reshape(devices, 16, tiles, per_tile, 16).transpose(2, 4, 1, 3, 0)
    result = filter_tiles(devices, blocks, tiles, False, data.reshape(tiles, 16, 16, LANES))
    field = result[:32].reshape(2, 16, 16, per_tile, devices).transpose(4, 0, 2, 3, 1)
    field = field.reshape(devices, 32, per_tile * 16)
    sums = jnp.broadcast_to(result[32, :ITERS, : per_tile * 16][None], (devices, ITERS, per_tile * 16))
    result = lax.all_to_all(jnp.concatenate([field, sums], axis=1), "rows", 0, 0)
    field = result[:, :32].reshape(devices, 2, 16, per_tile * 16).transpose(1, 2, 0, 3).reshape(2, 16, width)
    profile = result[:, 32:, 0].reshape(width // 128, -1, ITERS).sum(1).T
    return field, profile * scale


def solution(mesh):
    return jax.shard_map(
        per_device,
        mesh=mesh,
        in_specs=(P(("groups", "rows"), None),),
        out_specs=(P(None, ("groups", "rows"), None), P("groups", None)),
        check_vma=False,
    )
```

profile of v0, /device:TPU:0, one launch (start us, length us, event | category | flops | bytes accessed | tf_op | source)
XLA Modules:
  0.0 49.4 jit_solution(17253909981842972279)
XLA Ops:
  0.6 0.0 copy-start
  0.7 0.9 %copy-done = f32[16,2048]{1,0:T(8,128)S(1)} copy-done((f32[16,2048]{1,0:T(8,128)S(1)}, f32[16,2048]{1,0:T(8,128)}, u32[]{:S(2)}) %copy-start) | copy-done | bytes 131096
  1.6 17.3 %all_to_all.10.in_ref = f32[16,32,128]{2,1,0:T(8,128)} all-to-all(f32[16,32,128]{2,1,0:T(8,128)S(1)} %pad_maximum_fusion), channel_id=1, replica_groups=mesh['groups'=2,'rows'=16] {'rows'}, dimensions={0} | all-to-all | bytes 524288 | tf_op jit(solution)/shard_map/all_to_all | solution.py:341
  19.0 14.4 %filter_tiles.1 = f32[16,40,128]{2,1,0:T(8,128)} custom-call(f32[16,32,128]{2,1,0:T(8,128)} %all_to_all.10.in_ref), custom_call_target="tpu_custom_call" | custom-call | tf_op jit(solution)/shard_map/filter_tiles/pallas_call | solution.py:297
  33.4 14.6 %all_to_all.11 = f32[16,40,128]{2,1,0:T(8,128)S(1)} all-to-all(f32[16,40,128]{2,1,0:T(8,128)} %filter_tiles.1), channel_id=1, replica_groups=mesh['groups'=2,'rows'=16] {'rows'}, dimensions={0} | all-to-all | bytes 655360 | tf_op jit(solution)/shard_map/all_to_all | solution.py:343
  47.9 0.7 %copy.11 = f32[16,3,1]{0,1,2:T(4,128)} copy(f32[16,3,1]{2,1,0:T(4,128)S(1)} %slice_multiply_fusion) | data formatting | bytes 384 | tf_op jit(solution)/shard_map/mul | solution.py:346
  48.6 0.7 %copy.16 = f32[16,2,2,8,128]{4,3,0,2,1:T(8,128)} copy(f32[16,2,2,8,128]{4,3,2,1,0:T(8,128)S(1)} %bitcast.17) | data formatting | bytes 524288 | tf_op jit(solution)/shard_map/reshape | solution.py:344
  (7 shorter events, 0.1 us)
Async XLA Ops:
  0.6 0.9 %copy-start = (f32[16,2048]{1,0:T(8,128)S(1)}, f32[16,2048]{1,0:T(8,128)}, u32[]{:S(2)}) copy-start(f32[16,2048]{1,0:T(8,128)} %param.1) | copy-start | bytes 393220
where the time goes:
time: 49.7 us; the launch traced here: 49.4 us
  blocking collectives  31.9 us (64%)
  Pallas kernels  14.4 us (29%)
  local copies, waits for them, and re-layouts  2.34 us (5%)
  between operations  0.67 us (1%)
    all_to_all x1, blocking collectives, per_device(): data = lax.all_to_all(data, 'rows', 0, 0)  17.3 us
    all_to_all x1, blocking collectives, per_device(): result = lax.all_to_all(result, 'rows', 0, 0)  14.6 us
    pallas_call x1, Pallas kernels, filter_tiles(): pl.pallas_call(body, out_shape=jax.ShapeDtypeStruct(shape, jnp.float32),...  14.4 us

commit v1 on v0

--- a/solution.py
+++ b/solution.py
@@ -84,30 +84,30 @@
     return 1.0 - abs(t - 15.5) / 16.0
 
 
-def filter_kernel(slabs, blocks, tiles, packed, in_ref, out_ref, zr, zi, yr, yi, wr, wi, gain):
+def filter_kernel(slabs, blocks, tiles, packed, in_ref, out_ref, zr, zi, ur, ui, vr, vi, pr, pi, qr, qi, gain, turn):
     tile = lax.axis_index("rows")
     per_tile = LANES // slabs
+    ring = tiles * per_tile
     lane = lax.broadcasted_iota(jnp.int32, (8, LANES), 1)
     sub = lax.broadcasted_iota(jnp.int32, (8, LANES), 0)
-    slab = lane % slabs
-    not_last = slab != slabs - 1
-    not_first = slab != 0
+    not_last = lane % slabs != slabs - 1
+    not_first = lane % slabs != 0
     place = lane // slabs
 
     def inside(h, step):
-        position = (h * per_tile + place + step) % (tiles * per_tile)
-        relative = jnp.where(position < blocks + HALO, position, position - tiles * per_tile)
+        position = (h * per_tile + place + step) % ring
+        relative = jnp.where(position < blocks + HALO, position, position - ring)
         column = tile * blocks + relative
         return jnp.where((column >= 0) & (column < slabs * blocks), 1.0, 0.0)
 
     here = [inside(h, 0) for h in range(tiles)]
     both = [here[h] * inside(h, 1) for h in range(tiles)]
 
-    def right(values):
+    def right(values, active):
         if per_tile == 1:
-            return [values[(h + 1) % tiles] for h in range(tiles)]
+            return [values[(h + 1) % tiles] for h in active]
         moved = [pltpu.roll(v, LANES - slabs, 1) for v in values]
-        return [jnp.where(lane < LANES - slabs, moved[h], moved[(h + 1) % tiles]) for h in range(tiles)]
+        return [jnp.where(lane < LANES - slabs, moved[h], moved[(h + 1) % tiles]) for h in active]
 
     def left(values):
         if per_tile == 1:
@@ -132,7 +132,7 @@
                 zr[h * 16 + s, g * 8 : g * 8 + 8, :] = cosine * here[h]
                 zi[h * 16 + s, g * 8 : g * 8 + 8, :] = sine * here[h]
 
-    def measure_z():
+    def measure_z(active):
         total = jnp.zeros((8, LANES), jnp.float32)
         energy = [jnp.zeros((8, LANES), jnp.float32) for _ in range(tiles)]
         for h in range(1, tiles):
@@ -142,23 +142,24 @@
                     im = zi[h * 16 + s, g * 8 : g * 8 + 8, :]
                     energy[h] = energy[h] + (re * re + im * im)
 
-        def column(s, shifted):
+        def column(s):
             halves = []
             for ref in (zr, zi):
-                top = ref[s, 0:8, :]
-                low = ref[s, 8:16, :]
-                if shifted:
-                    top = right([ref[h * 16, 0:8, :] for h in range(tiles)])[0]
-                    low = right([ref[h * 16, 8:16, :] for h in range(tiles)])[0]
-                turned = [pltpu.roll(v, 7, 0) for v in (top, low, below(top))]
-                halves.append((top, low, jnp.where(sub < 7, turned[0], turned[1]), jnp.where(sub < 7, turned[1], turned[2])))
+                if s < 16:
+                    top = ref[s, 0:8, :]
+                    low = ref[s, 8:16, :]
+                else:
+                    top = right([ref[h * 16, 0:8, :] for h in range(tiles)], (0,))[0]
+                    low = right([ref[h * 16, 8:16, :] for h in range(tiles)], (0,))[0]
+                moved = [pltpu.roll(v, 7, 0) for v in (top, low, below(top))]
+                halves.append((top, low, jnp.where(sub < 7, moved[0], moved[1]), jnp.where(sub < 7, moved[1], moved[2])))
             (r0, r1, r0d, r1d), (i0, i1, i0d, i1d) = halves
             vertical = (i0 * r0d - r0 * i0d, i1 * r1d - r1 * i1d)
             return (r0, i0, r0d, i0d), (r1, i1, r1d, i1d), vertical
 
-        current = column(0, False)
+        current = column(0)
         for s in range(16):
-            following = column(s + 1, False) if s < 15 else column(0, True)
+            following = column(s + 1)
             for g in range(2):
                 r, i, rd, idn = current[g]
                 rn, in_, rdn, idnn = following[g]
@@ -170,125 +171,158 @@
             current = following
         summed = [jnp.broadcast_to(jnp.sum(e, axis=0, keepdims=True), (8, LANES)) for e in energy]
         tall = [e + below(e) for e in summed]
-        wide = right(tall)
-        for h in range(tiles):
-            gain[h * 8 : h * 8 + 8, :] = 1.0 / ((tall[h] + wide[h]) + EPS)
-        return jnp.sum(total)
-
-    def forward_columns(g):
+        wide = right(tall, active)
+        return jnp.sum(total), [1.0 / ((tall[h] + w) + EPS) for h, w in zip(active, wide)]
+
+    def sharing(h, needed):
+        places = {w % ring - h * per_tile for w in needed}
+        places = {p for p in places if 0 <= p < per_tile}
+        group = 1
+        for k in (2, 4):
+            if per_tile % k == 0:
+                taken = {(p + j * (per_tile // k)) % per_tile for p in places for j in range(k)}
+                group = k if len(taken) == k * len(places) else group
+        masks = []
+        for k in range(1, group):
+            mask = place < 0
+            for p in places:
+                mask = mask | (place == (p + k * (per_tile // group)) % per_tile)
+            masks.append(mask)
+        return masks
+
+    def merged(values, masks):
+        result = values[0]
+        for k, mask in enumerate(masks):
+            result = jnp.where(mask, pltpu.roll(values[k + 1], (k + 1) * LANES // (len(masks) + 1), 1), result)
+        return result
+
+    def forward_columns(plans, g):
         rows = pl.ds(pl.multiple_of(g * 8, 8), 8)
-        first = [[None] * 16 for _ in range(tiles)]
-        second = [[None] * 16 for _ in range(tiles)]
+        active = [h for h, _ in plans]
+        near = {h: [] for h in active}
+        far = {h: [] for h in active}
         for s in range(16):
             re = [zr[h * 16 + s, rows, :] for h in range(tiles)]
             im = [zi[h * 16 + s, rows, :] for h in range(tiles)]
-            for h, (a, b) in enumerate(zip(right(re), right(im))):
-                first[h][s] = (re[h], im[h])
-                second[h][s] = (a, b)
-        for h in range(tiles):
-            sums = [plus(a, b) for a, b in zip(first[h], second[h])]
-            differences = [rotated(minus(a, b), s, 32, -1) for s, (a, b) in enumerate(zip(first[h], second[h]))]
-            for parity, half in enumerate((sums, differences)):
-                for m, (re, im) in enumerate(fft(half, -1)):
-                    at = pl.ds((h * 32 + 2 * m + parity) * 17 + g * 8, 8)
-                    yr[at, :] = re
-                    yi[at, :] = im
-
-    def windows(unit):
-        h = unit // 4
-        q = unit % 4
-        base = (h * 32 + q * 8) * 17
-        scale = gain[pl.ds(pl.multiple_of(h * 8, 8), 8), :]
-        first = []
-        second = []
-        for t in range(16):
-            at = pl.ds(base + t, 8, stride=17)
-            re = yr[at, :]
-            im = yi[at, :]
-            first.append((re, im))
-            second.append((below(re), below(im)))
-        sums = [plus(a, b) for a, b in zip(first, second)]
-        differences = [rotated(minus(a, b), t, 32, -1) for t, (a, b) in enumerate(zip(first, second))]
+            for h, a, b in zip(active, right(re, active), right(im, active)):
+                near[h].append((re[h], im[h]))
+                far[h].append((a, b))
+        for h, masks in plans:
+            group = len(masks) + 1
+            even = fft([plus(a, b) for a, b in zip(near[h], far[h])], -1)
+            odd = fft([rotated(minus(a, b), s, 32, -1) for s, (a, b) in enumerate(zip(near[h], far[h]))], -1)
+            for row in range(32 // group):
+                sources = [(row // 8 * group + k) * 8 + row % 8 for k in range(group)]
+                values = [(even, odd)[l % 2][l // 2] for l in sources]
+                value = tuple(merged([v[part] for v in values], masks) for part in range(2))
+                following = (below(value[0]), below(value[1]))
+                at = pl.ds((h * 32 + row) * 17 + g * 8, 8)
+                ur[at, :], ui[at, :] = plus(value, following)
+                vr[at, :], vi[at, :] = minus(value, following)
+
+    def windows(h, unit):
+        scale = gain[h * 8 : h * 8 + 8, :]
+        at = [pl.ds((h * 32 + unit * 8) * 17 + t, 8, stride=17) for t in range(16)]
         back = []
-        for half in (sums, differences):
+        for parity, (a, b) in enumerate(((ur, ui), (vr, vi))):
+            values = [(a[x, :], b[x, :]) for x in at]
+            if parity:
+                values = [rotated(v, t, 32, -1) for t, v in enumerate(values)]
             filtered = []
-            for re, im in fft(half, -1):
-                power = (re * re + im * im) * scale
-                factor = lax.rsqrt(lax.rsqrt(power))
+            for re, im in fft(values, -1):
+                factor = lax.rsqrt(lax.rsqrt((re * re + im * im) * scale))
                 filtered.append((re * factor, im * factor))
             back.append(fft(filtered, 1))
         for t in range(16):
-            even = back[0][t]
             odd = rotated(back[1][t], t, 32, 1)
-            upper = plus(even, odd)
-            lower = minus(even, odd)
-            at = pl.ds((h * 16 + t) * 33 + q * 8, 8)
-            wr[at, :] = upper[0] * (ramp(t) / 32) + above(lower[0] * (ramp(t + 16) / 32))
-            wi[at, :] = upper[1] * (ramp(t) / 32) + above(lower[1] * (ramp(t + 16) / 32))
-
-    def inverse_columns(g):
+            upper = plus(back[0][t], odd)
+            lower = minus(back[0][t], odd)
+            at = pl.ds((h * 16 + t) * 33 + unit * 8, 8)
+            pr[at, :], pi[at, :] = (v * (ramp(t) / 32) for v in upper)
+            qr[at, :], qi[at, :] = (v * (ramp(t + 16) / 32) for v in lower)
+
+    def inverse_columns(plans, g):
         rows = pl.ds(pl.multiple_of(g * 8, 8), 8)
         kept = []
         passed = []
-        for h in range(tiles):
-            back = []
-            for parity in range(2):
-                values = []
-                for m in range(16):
-                    at = pl.ds((h * 16 + g * 8) * 33 + 2 * m + parity, 8, stride=33)
-                    values.append((wr[at, :], wi[at, :]))
-                back.append(fft(values, 1))
+        for h, masks in plans:
+            group = len(masks) + 1
+            values = [None] * 32
+            for row in range(32 // group):
+                at = pl.ds((h * 16 + g * 8) * 33 + row, 8, stride=33)
+                value = (pr[at, :] + above(qr[at, :]), pi[at, :] + above(qi[at, :]))
+                for k in range(group):
+                    l = (row // 8 * group + k) * 8 + row % 8
+                    values[l] = tuple(pltpu.roll(v, LANES - k * LANES // group, 1) if k else v for v in value)
+            even = fft(values[0::2], 1)
+            odd = fft(values[1::2], 1)
             own = []
             other = []
             for s in range(16):
-                odd = rotated(back[1][s], s, 32, 1)
-                near = here[h] * (ramp(s) / 32)
-                far = both[h] * (ramp(s + 16) / 32)
-                a = plus(back[0][s], odd)
-                b = minus(back[0][s], odd)
-                own.append((a[0] * near, a[1] * near))
-                other.append((b[0] * far, b[1] * far))
+                turned = rotated(odd[s], s, 32, 1)
+                weight = here[h] * (ramp(s) / 32)
+                own.append(tuple(v * weight for v in plus(even[s], turned)))
+                weight = both[h] * (ramp(s + 16) / 32)
+                other.append(tuple(v * weight for v in minus(even[s], turned)))
             kept.append(own)
             passed.append(other)
         for s in range(16):
             for part, ref in enumerate((zr, zi)):
-                arrived = left([passed[h][s][part] for h in range(tiles)])
-                for h in range(tiles):
-                    ref[h * 16 + s, rows, :] = kept[h][s][part] + arrived[h]
+                if len(plans) == tiles:
+                    arrived = left([passed[h][s][part] for h in range(tiles)])
+                    for h in range(tiles):
+                        ref[h * 16 + s, rows, :] = kept[h][s][part] + arrived[h]
+                else:
+                    ref[s, rows, :] = kept[0][s][part]
+                    ref[16 + s, rows, :] = pltpu.roll(passed[0][s][part], slabs, 1)
 
     def run(count, body):
         lax.fori_loop(0, count, lambda i, c: (body(i), c)[1], 0)
 
-    def iteration(step, carry):
-        total = measure_z()
-        out_ref_row(step, total)
-        run(2, forward_columns)
-        run(4 * tiles, windows)
-        run(2, inverse_columns)
-        return carry
-
-    if packed:
-
-        def out_ref_row(step, total):
-            for a in range(16):
-                out_ref[a, pl.ds(32 + step, 1), :] = jnp.full((1, LANES), total)
-
-    else:
-
-        def out_ref_row(step, total):
-            out_ref[32, pl.ds(step, 1), :] = jnp.full((1, LANES), total)
-
-    lax.fori_loop(0, ITERS, iteration, 0)
-
+    totals = []
+    for step in range(ITERS):
+        before = ITERS - step - (1 if packed else 0)
+        needed = range(-before, blocks + ITERS - 1 - step)
+        active = range(1 if packed and step == ITERS - 1 else tiles)
+        plans = [(h, sharing(h, needed)) for h in active]
+        total, gains = measure_z(active)
+        totals.append(total)
+        for (h, masks), value in zip(plans, gains):
+            gain[h * 8 : h * 8 + 8, :] = merged([value] * 4, masks)
+        run(2, functools.partial(forward_columns, plans))
+        for h, masks in plans:
+            run(4 // (len(masks) + 1), functools.partial(windows, h))
+        run(2, functools.partial(inverse_columns, plans))
+
+    if not packed:
+        for step, total in enumerate(totals):
+            out_ref[32, step : step + 1, :] = jnp.full((1, LANES), total)
+        for part, ref in enumerate((zr, zi)):
+            for s in range(16):
+                out_ref[part * 16 + s, :, :] = ref[s, :, :]
+        return
+
+    spill = []
     for part, ref in enumerate((zr, zi)):
         for g in range(2):
-            values = [ref[s, g * 8 : g * 8 + 8, :] for s in range(16)]
-            if packed:
-                for a, value in enumerate(swap_bits(values, lane)):
-                    out_ref[a, part * 16 + g * 8 : part * 16 + g * 8 + 8, :] = value
-            else:
-                for s, value in enumerate(values):
-                    out_ref[part * 16 + s, g * 8 : g * 8 + 8, :] = value
+            own = [ref[s, g * 8 : g * 8 + 8, :] for s in range(16)]
+            other = [ref[16 + s, g * 8 : g * 8 + 8, :] for s in range(16)]
+            values = [a + jnp.where(place > 0, b, 0.0) for a, b in zip(own, other)]
+            for a, value in enumerate(swap_bits(values, lane)):
+                out_ref[a, part * 16 + g * 8 : part * 16 + g * 8 + 8, :] = value
+            for q in range(2):
+                pack = other[8 * q]
+                for j in range(1, 8):
+                    pack = jnp.where(place == j, pltpu.roll(other[8 * q + j], j * slabs, 1), pack)
+                spill.append(pack)
+    turned = jnp.concatenate(spill + spill, axis=0).T
+    for j in range(8):
+        turn[j * 17 : j * 17 + 16, :] = turned[j * 16 : j * 16 + 16, :]
+    sums = jnp.zeros((8, LANES), jnp.float32)
+    for step, total in enumerate(totals):
+        sums = jnp.where((sub == step) & (lane == 64 + tile), total, sums)
+    for a in range(16):
+        out_ref[a, 32:40, :] = jnp.where(lane < 64, turn[pl.ds(a, 8, stride=17), :], sums)
 
 
 def filter_tiles(slabs, blocks, tiles, packed, data):
@@ -300,10 +334,46 @@
         in_specs=[pl.BlockSpec(memory_space=pltpu.VMEM)],
         out_specs=pl.BlockSpec(memory_space=pltpu.VMEM),
         scratch_shapes=[pltpu.VMEM((tiles * 16, 16, LANES), jnp.float32)] * 2
-        + [pltpu.VMEM((tiles * 32 * 17 + 8, LANES), jnp.float32)] * 2
-        + [pltpu.VMEM((tiles * 16 * 33 + 8, LANES), jnp.float32)] * 2
-        + [pltpu.VMEM((tiles * 8, LANES), jnp.float32)],
+        + [pltpu.VMEM((tiles * 32 * 17 + 8, LANES), jnp.float32)] * 4
+        + [pltpu.VMEM((tiles * 16 * 33 + 8, LANES), jnp.float32)] * 4
+        + [pltpu.VMEM((tiles * 8, LANES), jnp.float32), pltpu.VMEM((136, LANES), jnp.float32)],
+        compiler_params=pltpu.CompilerParams(vmem_limit_bytes=16 << 20),
         name="filter_tiles",
+    )(data)
+
+
+def finish_kernel(scale, in_ref, field_ref, profile_ref):
+    lane = lax.broadcasted_iota(jnp.int32, (8, LANES), 1)
+    extras = [in_ref[c, 32:40, :] for c in range(16)]
+    sums = functools.reduce(jnp.add, extras)
+    profile_ref[...] = pltpu.roll(sums, 64, 1)[:ITERS, :16] * scale
+    turned = jnp.concatenate(extras, axis=0).T
+    low = (lane & 8) == 0
+    for part in range(2):
+        for g in range(2):
+            first = (part * 2 + g) * 16
+            a = turned[first : first + 8]
+            b = turned[first + 8 : first + 16]
+            pairs = (jnp.where(low, a, pltpu.roll(b, 8, 1)), jnp.where(low, pltpu.roll(a, LANES - 8, 1), b))
+            for c in range(16):
+                value = in_ref[c, part * 16 + g * 8 : part * 16 + g * 8 + 8, :]
+                if c:
+                    spill = pltpu.roll(pairs[(c - 1) % 2], (LANES - (c - 1) // 2 * 16) % LANES, 1)
+                    value = value + jnp.where(lane < 16, spill, 0.0)
+                field_ref[part, g * 8 : g * 8 + 8, c * LANES : (c + 1) * LANES] = value
+
+
+def finish(scale, data):
+    return pl.pallas_call(
+        functools.partial(finish_kernel, scale),
+        out_shape=(
+            jax.ShapeDtypeStruct((2, 16, 16 * LANES), jnp.float32),
+            jax.ShapeDtypeStruct((ITERS, 16), jnp.float32),
+        ),
+        in_specs=[pl.BlockSpec(memory_space=pltpu.VMEM)],
+        out_specs=[pl.BlockSpec(memory_space=pltpu.VMEM)] * 2,
+        compiler_params=pltpu.CompilerParams(vmem_limit_bytes=8 << 20),
+        name="finish",
     )(data)
 
 
@@ -341,9 +411,7 @@
         data = lax.all_to_all(data, "rows", 0, 0)
         result = filter_tiles(devices, blocks, tiles, True, data)
         result = lax.all_to_all(result, "rows", 0, 0)
-        field = result[:, :32].reshape(devices, 2, 16, LANES).transpose(1, 2, 0, 3).reshape(2, 16, width)
-        profile = result[:, 32 : 32 + ITERS, 0].T
-        return field, profile * scale
+        return finish(scale, result)
     tiles = -(-(blocks + 2 * HALO) // per_tile)
     data = lax.all_to_all(ring_of_blocks(phase, devices, blocks, tiles), "rows", 0, 0)
     data = data.reshape(devices, 16, tiles, per_tile, 16).transpose(2, 4, 1, 3, 0)

time: 49.7 us -> 43.9 us (0.88)
  Pallas kernels: 14.4 us -> 11 us
  local copies, waits for them, and re-layouts: 2.34 us -> 0.92 us
  blocking collectives: 31.9 us -> 31 us
    pallas_call x1, Pallas kernels: 14.4 us -> 10.1 us  [filter_tiles(): pl.pallas_call(body, out_shape=jax.ShapeDtypeStruct(shape, jnp.float32),...]
    pallas_call x0 -> x1, Pallas kernels: none -> 0.98 us  [finish(): pl.pallas_call(functools.partial(finish_kernel, scale), out_shape=(jax.Sh...]
    all_to_all x1, blocking collectives: 14.6 us -> 13.7 us  [per_device(): result = lax.all_to_all(result, 'rows', 0, 0)]
    reshape x1 -> x0, local copies, waits for them, and re-layouts: 0.72 us -> none  [per_device(): result[:, :32].reshape(devices, 2, 16, LANES).transpose(1, 2, 0, 3)]
    mul x1 -> x0, local copies, waits for them, and re-layouts: 0.68 us -> none  [per_device(): return (field, profile * scale)]
where the time goes in v1:
time: 43.9 us; the launch traced here: 43.7 us
  blocking collectives  31 us (71%)
  Pallas kernels  11 us (25%)
  local copies, waits for them, and re-layouts  0.92 us (2%)
  between operations  0.67 us (2%)
    all_to_all x1, blocking collectives, per_device(): data = lax.all_to_all(data, 'rows', 0, 0)  17.2 us
    all_to_all x1, blocking collectives, per_device(): result = lax.all_to_all(result, 'rows', 0, 0)  13.7 us
    pallas_call x1, Pallas kernels, filter_tiles(): pl.pallas_call(body, out_shape=jax.ShapeDtypeStruct(shape, jnp.float32),...  10.1 us
    pallas_call x1, Pallas kernels, finish(): pl.pallas_call(functools.partial(finish_kernel, scale), out_shape=(jax.Sh...  0.98 us
    unnamed x2, local copies, waits for them, and re-layouts  0.89 us

profile of v1, /device:TPU:0, one launch (start us, length us, event | category | flops | bytes accessed | tf_op | source)
XLA Modules:
  0.0 43.7 jit_solution(13636327210794283687)
XLA Ops:
  0.6 0.0 copy-start
  0.7 0.9 %copy-done = f32[16,2048]{1,0:T(8,128)S(1)} copy-done((f32[16,2048]{1,0:T(8,128)S(1)}, f32[16,2048]{1,0:T(8,128)}, u32[]{:S(2)}) %copy-start) | copy-done | bytes 131096
  1.6 17.2 %all_to_all.10.in_ref = f32[16,32,128]{2,1,0:T(8,128)S(1)} all-to-all(f32[16,32,128]{2,1,0:T(8,128)S(1)} %pad_maximum_fusion), channel_id=1, replica_groups=mesh['groups'=2,'rows'=16] {'rows'}, dimensions={0} | all-to-all | bytes 524288 | tf_op jit(solution)/shard_map/all_to_all | solution.py:411
  18.9 10.1 %filter_tiles.1 = f32[16,40,128]{2,1,0:T(8,128)S(1)} custom-call(f32[16,32,128]{2,1,0:T(8,128)S(1)} %all_to_all.10.in_ref), custom_call_target="tpu_custom_call" | custom-call | tf_op jit(solution)/shard_map/filter_tiles/pallas_call | solution.py:331
  28.9 13.7 %all_to_all.11.in_ref = f32[16,40,128]{2,1,0:T(8,128)S(1)} all-to-all(f32[16,40,128]{2,1,0:T(8,128)S(1)} %filter_tiles.1), channel_id=1, replica_groups=mesh['groups'=2,'rows'=16] {'rows'}, dimensions={0} | all-to-all | bytes 655360 | tf_op jit(solution)/shard_map/all_to_all | solution.py:413
  42.7 1.0 %finish.1 = (f32[2,16,2048]{2,1,0:T(8,128)}, f32[3,16]{1,0:T(4,128)}) custom-call(f32[16,40,128]{2,1,0:T(8,128)S(1)} %all_to_all.11.in_ref), custom_call_target="tpu_custom_call" | custom-call | tf_op jit(solution)/shard_map/finish/pallas_call | solution.py:367
  (5 shorter events, 0.1 us)
Async XLA Ops:
  0.6 0.9 %copy-start = (f32[16,2048]{1,0:T(8,128)S(1)}, f32[16,2048]{1,0:T(8,128)}, u32[]{:S(2)}) copy-start(f32[16,2048]{1,0:T(8,128)} %param.1) | copy-start | bytes 393220

commit v2 on v1

--- a/solution.py
+++ b/solution.py
@@ -84,7 +84,9 @@
     return 1.0 - abs(t - 15.5) / 16.0
 
 
-def filter_kernel(slabs, blocks, tiles, packed, in_ref, out_ref, zr, zi, ur, ui, vr, vi, pr, pi, qr, qi, gain, turn):
+def filter_kernel(
+    slabs, blocks, tiles, packed, in_ref, out_ref, zr, zi, yr, yi, ur, ui, vr, vi, wr, wi, pr, pi, qr, qi, energy, gain, sums, turn
+):
     tile = lax.axis_index("rows")
     per_tile = LANES // slabs
     ring = tiles * per_tile
@@ -121,58 +123,24 @@
     def above(value):
         return jnp.where(not_first, pltpu.roll(value, 1, 1), 0.0)
 
+    def keep(h, s, g, value, power):
+        for part, ref in enumerate((zr, zi)):
+            ref[h * 16 + s, pl.ds(g * 8, 8), :] = value[part]
+            if h == 0 or s == 0:
+                ref[h * 16 + s, pl.ds(16 + g, 1), :] = below(value[part])[0:1]
+        return power + (value[0] * value[0] + value[1] * value[1])
+
     for h in range(tiles):
         for g in range(2):
             if packed:
                 phases = swap_bits([in_ref[a, h * 16 + g * 8 : h * 16 + g * 8 + 8, :] for a in range(16)], lane)
             else:
                 phases = [in_ref[h, s, g * 8 : g * 8 + 8, :] for s in range(16)]
+            power = jnp.zeros((8, LANES), jnp.float32)
             for s in range(16):
                 cosine, sine = cos_sin(phases[s])
-                zr[h * 16 + s, g * 8 : g * 8 + 8, :] = cosine * here[h]
-                zi[h * 16 + s, g * 8 : g * 8 + 8, :] = sine * here[h]
-
-    def measure_z(active):
-        total = jnp.zeros((8, LANES), jnp.float32)
-        energy = [jnp.zeros((8, LANES), jnp.float32) for _ in range(tiles)]
-        for h in range(1, tiles):
-            for s in range(16):
-                for g in range(2):
-                    re = zr[h * 16 + s, g * 8 : g * 8 + 8, :]
-                    im = zi[h * 16 + s, g * 8 : g * 8 + 8, :]
-                    energy[h] = energy[h] + (re * re + im * im)
-
-        def column(s):
-            halves = []
-            for ref in (zr, zi):
-                if s < 16:
-                    top = ref[s, 0:8, :]
-                    low = ref[s, 8:16, :]
-                else:
-                    top = right([ref[h * 16, 0:8, :] for h in range(tiles)], (0,))[0]
-                    low = right([ref[h * 16, 8:16, :] for h in range(tiles)], (0,))[0]
-                moved = [pltpu.roll(v, 7, 0) for v in (top, low, below(top))]
-                halves.append((top, low, jnp.where(sub < 7, moved[0], moved[1]), jnp.where(sub < 7, moved[1], moved[2])))
-            (r0, r1, r0d, r1d), (i0, i1, i0d, i1d) = halves
-            vertical = (i0 * r0d - r0 * i0d, i1 * r1d - r1 * i1d)
-            return (r0, i0, r0d, i0d), (r1, i1, r1d, i1d), vertical
-
-        current = column(0)
-        for s in range(16):
-            following = column(s + 1)
-            for g in range(2):
-                r, i, rd, idn = current[g]
-                rn, in_, rdn, idnn = following[g]
-                energy[0] = energy[0] + (r * r + i * i)
-                across = i * rn - r * in_
-                across_down = idn * rdn - rd * idnn
-                loop = (across - across_down) + (following[2][g] - current[2][g])
-                total = total + loop * loop
-            current = following
-        summed = [jnp.broadcast_to(jnp.sum(e, axis=0, keepdims=True), (8, LANES)) for e in energy]
-        tall = [e + below(e) for e in summed]
-        wide = right(tall, active)
-        return jnp.sum(total), [1.0 / ((tall[h] + w) + EPS) for h, w in zip(active, wide)]
+                power = keep(h, s, g, (cosine * here[h], sine * here[h]), power)
+            energy[h * 16 + g * 8 : h * 16 + g * 8 + 8, :] = power
 
     def sharing(h, needed):
         places = {w % ring - h * per_tile for w in needed}
@@ -196,9 +164,20 @@
             result = jnp.where(mask, pltpu.roll(values[k + 1], (k + 1) * LANES // (len(masks) + 1), 1), result)
         return result
 
-    def forward_columns(plans, g):
+    def window_gains(plans):
+        both_rows = [energy[h * 16 : h * 16 + 8, :] + energy[h * 16 + 8 : h * 16 + 16, :] for h in range(tiles)]
+        blockwise = [jnp.broadcast_to(jnp.sum(e, axis=0, keepdims=True), (8, LANES)) for e in both_rows]
+        tall = [e + below(e) for e in blockwise]
+        for unit, ((h, masks, first, count), wide) in enumerate(zip(plans, right(tall, [p[0] for p in plans]))):
+            value = merged([1.0 / ((tall[h] + wide) + EPS)] * 4, masks)
+            for j in range(count):
+                gain[(first + j) * 8 : (first + j) * 8 + 8, :] = value
+
+    def forward_columns(step, plans, g):
         rows = pl.ds(pl.multiple_of(g * 8, 8), 8)
-        active = [h for h, _ in plans]
+        under = pl.ds(g * 8 + 1, 8)
+        active = [p[0] for p in plans]
+        window_gains(plans)
         near = {h: [] for h in active}
         far = {h: [] for h in active}
         for s in range(16):
@@ -207,22 +186,63 @@
             for h, a, b in zip(active, right(re, active), right(im, active)):
                 near[h].append((re[h], im[h]))
                 far[h].append((a, b))
-        for h, masks in plans:
+        for h, masks, first, count in plans:
             group = len(masks) + 1
             even = fft([plus(a, b) for a, b in zip(near[h], far[h])], -1)
             odd = fft([rotated(minus(a, b), s, 32, -1) for s, (a, b) in enumerate(zip(near[h], far[h]))], -1)
-            for row in range(32 // group):
+            for row in range(8 * count):
                 sources = [(row // 8 * group + k) * 8 + row % 8 for k in range(group)]
                 values = [(even, odd)[l % 2][l // 2] for l in sources]
                 value = tuple(merged([v[part] for v in values], masks) for part in range(2))
+                at = pl.ds((first * 8 + row) * 17 + g * 8, 8)
+                if first == 0 and row < 8:
+                    following = (below(value[0]), below(value[1]))
+                    ur[at, :], ui[at, :] = plus(value, following)
+                    vr[at, :], vi[at, :] = minus(value, following)
+                else:
+                    yr[at, :], yi[at, :] = value
+
+        def corner(s):
+            if s < 16:
+                return near[0][s], (zr[s, under, :], zi[s, under, :])
+            moved = [right([ref[h * 16, under, :] for h in range(tiles)], (0,))[0] for ref in (zr, zi)]
+            return far[0][0], tuple(moved)
+
+        def cross(a, b):
+            return a[1] * b[0] - a[0] * b[1]
+
+        total = jnp.zeros((8, LANES), jnp.float32)
+        here_, under_ = corner(0)
+        down = cross(here_, under_)
+        for s in range(16):
+            next_, next_under = corner(s + 1)
+            next_down = cross(next_, next_under)
+            loop = (cross(here_, next_) - cross(under_, next_under)) + (next_down - down)
+            total = total + loop * loop
+            here_, under_, down = next_, next_under, next_down
+        sums[pl.ds(pl.multiple_of(step * 16 + g * 8, 8), 8), :] = total
+
+    def split_rows(unit):
+        for row in range(8):
+            for g in range(2):
+                source = pl.ds((unit * 8 + row) * 17 + g * 8, 8)
+                at = pl.ds(row * 17 + g * 8, 8)
+                value = (yr[source, :], yi[source, :])
                 following = (below(value[0]), below(value[1]))
-                at = pl.ds((h * 32 + row) * 17 + g * 8, 8)
                 ur[at, :], ui[at, :] = plus(value, following)
                 vr[at, :], vi[at, :] = minus(value, following)
 
-    def windows(h, unit):
-        scale = gain[h * 8 : h * 8 + 8, :]
-        at = [pl.ds((h * 32 + unit * 8) * 17 + t, 8, stride=17) for t in range(16)]
+    def join_rows(unit):
+        for t in range(16):
+            source = pl.ds(t * 9, 8)
+            at = pl.ds((unit * 16 + t) * 9, 8)
+            wr[at, :] = pr[source, :] + above(qr[source, :])
+            wi[at, :] = pi[source, :] + above(qi[source, :])
+
+    def windows(unit):
+        join_rows(jnp.maximum(unit - 1, 0))
+        scale = gain[pl.ds(pl.multiple_of(unit * 8, 8), 8), :]
+        at = [pl.ds(t, 8, stride=17) for t in range(16)]
         back = []
         for parity, (a, b) in enumerate(((ur, ui), (vr, vi))):
             values = [(a[x, :], b[x, :]) for x in at]
@@ -233,24 +253,30 @@
                 factor = lax.rsqrt(lax.rsqrt((re * re + im * im) * scale))
                 filtered.append((re * factor, im * factor))
             back.append(fft(filtered, 1))
+        split_rows(unit + 1)
         for t in range(16):
             odd = rotated(back[1][t], t, 32, 1)
             upper = plus(back[0][t], odd)
             lower = minus(back[0][t], odd)
-            at = pl.ds((h * 16 + t) * 33 + unit * 8, 8)
+            at = pl.ds(t * 9, 8)
             pr[at, :], pi[at, :] = (v * (ramp(t) / 32) for v in upper)
             qr[at, :], qi[at, :] = (v * (ramp(t + 16) / 32) for v in lower)
 
-    def inverse_columns(plans, g):
+    def inverse_columns(plans, units, g):
         rows = pl.ds(pl.multiple_of(g * 8, 8), 8)
         kept = []
         passed = []
-        for h, masks in plans:
+        for h, masks, first, count in plans:
             group = len(masks) + 1
             values = [None] * 32
-            for row in range(32 // group):
-                at = pl.ds((h * 16 + g * 8) * 33 + row, 8, stride=33)
-                value = (pr[at, :] + above(qr[at, :]), pi[at, :] + above(qi[at, :]))
+            for row in range(8 * count):
+                unit = first + row // 8
+                if unit == units - 1:
+                    at = pl.ds(g * 72 + row % 8, 8, stride=9)
+                    value = (pr[at, :] + above(qr[at, :]), pi[at, :] + above(qi[at, :]))
+                else:
+                    at = pl.ds(unit * 144 + g * 72 + row % 8, 8, stride=9)
+                    value = (wr[at, :], wi[at, :])
                 for k in range(group):
                     l = (row // 8 * group + k) * 8 + row % 8
                     values[l] = tuple(pltpu.roll(v, LANES - k * LANES // group, 1) if k else v for v in value)
@@ -266,40 +292,44 @@
                 other.append(tuple(v * weight for v in minus(even[s], turned)))
             kept.append(own)
             passed.append(other)
+        if len(plans) == tiles:
+            power = [jnp.zeros((8, LANES), jnp.float32) for _ in range(tiles)]
+            for s in range(16):
+                arrived = [left([passed[h][s][part] for h in range(tiles)]) for part in range(2)]
+                for h in range(tiles):
+                    value = tuple(kept[h][s][part] + arrived[part][h] for part in range(2))
+                    power[h] = keep(h, s, g, value, power[h])
+            for h in range(tiles):
+                energy[pl.ds(pl.multiple_of(h * 16 + g * 8, 8), 8), :] = power[h]
+            return
         for s in range(16):
             for part, ref in enumerate((zr, zi)):
-                if len(plans) == tiles:
-                    arrived = left([passed[h][s][part] for h in range(tiles)])
-                    for h in range(tiles):
-                        ref[h * 16 + s, rows, :] = kept[h][s][part] + arrived[h]
-                else:
-                    ref[s, rows, :] = kept[0][s][part]
-                    ref[16 + s, rows, :] = pltpu.roll(passed[0][s][part], slabs, 1)
+                ref[s, rows, :] = kept[0][s][part]
+                ref[16 + s, rows, :] = pltpu.roll(passed[0][s][part], slabs, 1)
 
     def run(count, body):
         lax.fori_loop(0, count, lambda i, c: (body(i), c)[1], 0)
 
-    totals = []
     for step in range(ITERS):
         before = ITERS - step - (1 if packed else 0)
         needed = range(-before, blocks + ITERS - 1 - step)
-        active = range(1 if packed and step == ITERS - 1 else tiles)
-        plans = [(h, sharing(h, needed)) for h in active]
-        total, gains = measure_z(active)
-        totals.append(total)
-        for (h, masks), value in zip(plans, gains):
-            gain[h * 8 : h * 8 + 8, :] = merged([value] * 4, masks)
-        run(2, functools.partial(forward_columns, plans))
-        for h, masks in plans:
-            run(4 // (len(masks) + 1), functools.partial(windows, h))
-        run(2, functools.partial(inverse_columns, plans))
+        plans = []
+        units = 0
+        for h in range(1 if packed and step == ITERS - 1 else tiles):
+            masks = sharing(h, needed)
+            plans.append((h, masks, units, 4 // (len(masks) + 1)))
+            units += 4 // (len(masks) + 1)
+        run(2, functools.partial(forward_columns, step, plans))
+        run(units, windows)
+        run(2, functools.partial(inverse_columns, plans, units))
+    totals = [jnp.sum(sums[step * 16 : step * 16 + 8, :] + sums[step * 16 + 8 : step * 16 + 16, :]) for step in range(ITERS)]
 
     if not packed:
         for step, total in enumerate(totals):
             out_ref[32, step : step + 1, :] = jnp.full((1, LANES), total)
         for part, ref in enumerate((zr, zi)):
             for s in range(16):
-                out_ref[part * 16 + s, :, :] = ref[s, :, :]
+                out_ref[part * 16 + s, :, :] = ref[s, 0:16, :]
         return
 
     spill = []
@@ -318,11 +348,11 @@
     turned = jnp.concatenate(spill + spill, axis=0).T
     for j in range(8):
         turn[j * 17 : j * 17 + 16, :] = turned[j * 16 : j * 16 + 16, :]
-    sums = jnp.zeros((8, LANES), jnp.float32)
+    report = jnp.zeros((8, LANES), jnp.float32)
     for step, total in enumerate(totals):
-        sums = jnp.where((sub == step) & (lane == 64 + tile), total, sums)
+        report = jnp.where((sub == step) & (lane == 64 + tile), total, report)
     for a in range(16):
-        out_ref[a, 32:40, :] = jnp.where(lane < 64, turn[pl.ds(a, 8, stride=17), :], sums)
+        out_ref[a, 32:40, :] = jnp.where(lane < 64, turn[pl.ds(a, 8, stride=17), :], report)
 
 
 def filter_tiles(slabs, blocks, tiles, packed, data):
@@ -333,10 +363,12 @@
         out_shape=jax.ShapeDtypeStruct(shape, jnp.float32),
         in_specs=[pl.BlockSpec(memory_space=pltpu.VMEM)],
         out_specs=pl.BlockSpec(memory_space=pltpu.VMEM),
-        scratch_shapes=[pltpu.VMEM((tiles * 16, 16, LANES), jnp.float32)] * 2
-        + [pltpu.VMEM((tiles * 32 * 17 + 8, LANES), jnp.float32)] * 4
-        + [pltpu.VMEM((tiles * 16 * 33 + 8, LANES), jnp.float32)] * 4
-        + [pltpu.VMEM((tiles * 8, LANES), jnp.float32), pltpu.VMEM((136, LANES), jnp.float32)],
+        scratch_shapes=[pltpu.VMEM((tiles * 16, 24, LANES), jnp.float32)] * 2
+        + [pltpu.VMEM(((tiles * 4 + 1) * 136, LANES), jnp.float32)] * 2
+        + [pltpu.VMEM((136, LANES), jnp.float32)] * 4
+        + [pltpu.VMEM((tiles * 4 * 144, LANES), jnp.float32)] * 2
+        + [pltpu.VMEM((144, LANES), jnp.float32)] * 4
+        + [pltpu.VMEM((rows, LANES), jnp.float32) for rows in (tiles * 16, tiles * 32, ITERS * 16, 136)],
         compiler_params=pltpu.CompilerParams(vmem_limit_bytes=16 << 20),
         name="filter_tiles",
     )(data)

time: 43.9 us -> 42.4 us (0.966)
  Pallas kernels: 11 us -> 9.6 us
    pallas_call x1, Pallas kernels: 10.1 us -> 8.62 us  [filter_tiles(): pl.pallas_call(body, out_shape=jax.ShapeDtypeStruct(shape, jnp.float32),...]
where the time goes in v2:
time: 42.4 us; the launch traced here: 42.2 us
  blocking collectives  31 us (73%)
  Pallas kernels  9.6 us (23%)
  local copies, waits for them, and re-layouts  0.92 us (2%)
  between operations  0.67 us (2%)
    all_to_all x1, blocking collectives, per_device(): data = lax.all_to_all(data, 'rows', 0, 0)  17.2 us
    all_to_all x1, blocking collectives, per_device(): result = lax.all_to_all(result, 'rows', 0, 0)  13.7 us
    pallas_call x1, Pallas kernels, filter_tiles(): pl.pallas_call(body, out_shape=jax.ShapeDtypeStruct(shape, jnp.float32),...  8.62 us
    pallas_call x1, Pallas kernels, finish(): pl.pallas_call(functools.partial(finish_kernel, scale), out_shape=(jax.Sh...  0.98 us
    unnamed x2, local copies, waits for them, and re-layouts  0.89 us

profile of v2, /device:TPU:0, one launch (start us, length us, event | category | flops | bytes accessed | tf_op | source)
XLA Modules:
  0.0 42.2 jit_solution(2364423508022187053)
XLA Ops:
  0.6 0.0 copy-start
  0.7 0.9 %copy-done = f32[16,2048]{1,0:T(8,128)S(1)} copy-done((f32[16,2048]{1,0:T(8,128)S(1)}, f32[16,2048]{1,0:T(8,128)}, u32[]{:S(2)}) %copy-start) | copy-done | bytes 131096
  1.6 17.2 %all_to_all.10.in_ref = f32[16,32,128]{2,1,0:T(8,128)S(1)} all-to-all(f32[16,32,128]{2,1,0:T(8,128)S(1)} %pad_maximum_fusion), channel_id=1, replica_groups=mesh['groups'=2,'rows'=16] {'rows'}, dimensions={0} | all-to-all | bytes 524288 | tf_op jit(solution)/shard_map/all_to_all | solution.py:443
  18.9 8.6 %filter_tiles.1 = f32[16,40,128]{2,1,0:T(8,128)S(1)} custom-call(f32[16,32,128]{2,1,0:T(8,128)S(1)} %all_to_all.10.in_ref), custom_call_target="tpu_custom_call" | custom-call | tf_op jit(solution)/shard_map/filter_tiles/pallas_call | solution.py:361
  27.5 13.7 %all_to_all.11.in_ref = f32[16,40,128]{2,1,0:T(8,128)S(1)} all-to-all(f32[16,40,128]{2,1,0:T(8,128)S(1)} %filter_tiles.1), channel_id=1, replica_groups=mesh['groups'=2,'rows'=16] {'rows'}, dimensions={0} | all-to-all | bytes 655360 | tf_op jit(solution)/shard_map/all_to_all | solution.py:445
  41.2 1.0 %finish.1 = (f32[2,16,2048]{2,1,0:T(8,128)}, f32[3,16]{1,0:T(4,128)}) custom-call(f32[16,40,128]{2,1,0:T(8,128)S(1)} %all_to_all.11.in_ref), custom_call_target="tpu_custom_call" | custom-call | tf_op jit(solution)/shard_map/finish/pallas_call | solution.py:399
  (5 shorter events, 0.1 us)
Async XLA Ops:
  0.6 0.9 %copy-start = (f32[16,2048]{1,0:T(8,128)S(1)}, f32[16,2048]{1,0:T(8,128)}, u32[]{:S(2)}) copy-start(f32[16,2048]{1,0:T(8,128)} %param.1) | copy-start | bytes 393220

commit v3 on v2

--- a/solution.py
+++ b/solution.py
@@ -13,8 +13,8 @@
 LANES = 128
 HALO = 3
 
-SIN = (1.000000000e+00, -1.666666662e-01, 8.333330977e-03, -1.984086143e-04, 2.752528078e-06, -2.388938418e-08)
-COS = (9.999999998e-01, -4.999999936e-01, 4.166663620e-02, -1.388836069e-03, 2.476012736e-05, -2.605092951e-07)
+SIN = (9.99999996e-01, -1.66666580e-01, 8.33305053e-03, -1.98090400e-04, 2.60515161e-06)
+COS = (9.99999953e-01, -4.99999050e-01, 4.16635780e-02, -1.38536600e-03, 2.31530144e-05)
 
 
 def rotated(value, k, size, sign):
@@ -28,6 +28,8 @@
         return ((re + im) * half, (im - re) * half) if sign < 0 else ((re - im) * half, (im + re) * half)
     if 8 * k == 3 * size:
         return ((im - re) * half, (re + im) * -half) if sign < 0 else ((re + im) * -half, (re - im) * half)
+    if 2 * k > size:
+        return rotated((-re, -im), k - size // 2, size, sign)
     c = math.cos(2 * math.pi * k / size)
     s = sign * math.sin(2 * math.pi * k / size)
     return re * c - im * s, im * c + re * s
@@ -39,16 +41,40 @@
 
 def minus(a, b):
     return a[0] - b[0], a[1] - b[1]
+
+
+def quarter_turn(a, sign):
+    return (-a[1], a[0]) if sign > 0 else (a[1], -a[0])
+
+
+def join(one, three, size, sign):
+    quarter = size // 4
+    one = [rotated(one[k], k, size, sign) for k in range(quarter)]
+    three = [rotated(three[k], 3 * k, size, sign) for k in range(quarter)]
+    turned = [quarter_turn(minus(a, b), sign) for a, b in zip(one, three)]
+    return [plus(a, b) for a, b in zip(one, three)] + turned
 
 
 def fft(values, sign):
     size = len(values)
     if size == 1:
         return values
+    if size == 2:
+        return [plus(*values), minus(*values)]
     even = fft(values[0::2], sign)
-    odd = fft(values[1::2], sign)
-    turned = [rotated(odd[k], k, size, sign) for k in range(size // 2)]
-    return [plus(e, o) for e, o in zip(even, turned)] + [minus(e, o) for e, o in zip(even, turned)]
+    odd = join(fft(values[1::4], sign), fft(values[3::4], sign), size, sign)
+    return [plus(e, o) for e, o in zip(even, odd)] + [minus(e, o) for e, o in zip(even, odd)]
+
+
+def odd_outputs(differences):
+    one = []
+    three = []
+    for k in range(8):
+        turned = quarter_turn(differences[k + 8], -1)
+        one.append(rotated(plus(differences[k], turned), k, 32, -1))
+        three.append(rotated(minus(differences[k], turned), 3 * k, 32, -1))
+    pairs = zip(fft(one, -1), fft(three, -1))
+    return [value for pair in pairs for value in pair]
 
 
 def polynomial(coefficients, w):
@@ -66,26 +92,12 @@
     return cosine, jnp.where(x < 0, -sine, sine)
 
 
-def swap_bits(values, lane):
-    values = list(values)
-    bit = 1
-    while bit < len(values):
-        clear = (lane & bit) == 0
-        for p in range(len(values)):
-            if p & bit == 0:
-                low, high = values[p], values[p | bit]
-                values[p] = jnp.where(clear, low, pltpu.roll(high, bit, 1))
-                values[p | bit] = jnp.where(clear, pltpu.roll(low, LANES - bit, 1), high)
-        bit *= 2
-    return values
-
-
 def ramp(t):
     return 1.0 - abs(t - 15.5) / 16.0
 
 
 def filter_kernel(
-    slabs, blocks, tiles, packed, in_ref, out_ref, zr, zi, yr, yi, ur, ui, vr, vi, wr, wi, pr, pi, qr, qi, energy, gain, sums, turn
+    slabs, blocks, tiles, in_ref, out_ref, zr, zi, yr, yi, ur, ui, vr, vi, wr, wi, pr, pi, qr, qi, energy, gain, sums
 ):
     tile = lax.axis_index("rows")
     per_tile = LANES // slabs
@@ -132,10 +144,7 @@
 
     for h in range(tiles):
         for g in range(2):
-            if packed:
-                phases = swap_bits([in_ref[a, h * 16 + g * 8 : h * 16 + g * 8 + 8, :] for a in range(16)], lane)
-            else:
-                phases = [in_ref[h, s, g * 8 : g * 8 + 8, :] for s in range(16)]
+            phases = [in_ref[h, s, g * 8 : g * 8 + 8, :] for s in range(16)]
             power = jnp.zeros((8, LANES), jnp.float32)
             for s in range(16):
                 cosine, sine = cos_sin(phases[s])
@@ -292,30 +301,23 @@
                 other.append(tuple(v * weight for v in minus(even[s], turned)))
             kept.append(own)
             passed.append(other)
-        if len(plans) == tiles:
-            power = [jnp.zeros((8, LANES), jnp.float32) for _ in range(tiles)]
-            for s in range(16):
-                arrived = [left([passed[h][s][part] for h in range(tiles)]) for part in range(2)]
-                for h in range(tiles):
-                    value = tuple(kept[h][s][part] + arrived[part][h] for part in range(2))
-                    power[h] = keep(h, s, g, value, power[h])
+        power = [jnp.zeros((8, LANES), jnp.float32) for _ in range(tiles)]
+        for s in range(16):
+            arrived = [left([passed[h][s][part] for h in range(tiles)]) for part in range(2)]
             for h in range(tiles):
-                energy[pl.ds(pl.multiple_of(h * 16 + g * 8, 8), 8), :] = power[h]
-            return
-        for s in range(16):
-            for part, ref in enumerate((zr, zi)):
-                ref[s, rows, :] = kept[0][s][part]
-                ref[16 + s, rows, :] = pltpu.roll(passed[0][s][part], slabs, 1)
+                value = tuple(kept[h][s][part] + arrived[part][h] for part in range(2))
+                power[h] = keep(h, s, g, value, power[h])
+        for h in range(tiles):
+            energy[pl.ds(pl.multiple_of(h * 16 + g * 8, 8), 8), :] = power[h]
 
     def run(count, body):
         lax.fori_loop(0, count, lambda i, c: (body(i), c)[1], 0)
 
     for step in range(ITERS):
-        before = ITERS - step - (1 if packed else 0)
-        needed = range(-before, blocks + ITERS - 1 - step)
+        needed = range(step - ITERS, blocks + ITERS - 1 - step)
         plans = []
         units = 0
-        for h in range(1 if packed and step == ITERS - 1 else tiles):
+        for h in range(tiles):
             masks = sharing(h, needed)
             plans.append((h, masks, units, 4 // (len(masks) + 1)))
             units += 4 // (len(masks) + 1)
@@ -324,43 +326,18 @@
         run(2, functools.partial(inverse_columns, plans, units))
     totals = [jnp.sum(sums[step * 16 : step * 16 + 8, :] + sums[step * 16 + 8 : step * 16 + 16, :]) for step in range(ITERS)]
 
-    if not packed:
-        for step, total in enumerate(totals):
-            out_ref[32, step : step + 1, :] = jnp.full((1, LANES), total)
-        for part, ref in enumerate((zr, zi)):
-            for s in range(16):
-                out_ref[part * 16 + s, :, :] = ref[s, 0:16, :]
-        return
-
-    spill = []
+    for step, total in enumerate(totals):
+        out_ref[32, step : step + 1, :] = jnp.full((1, LANES), total)
     for part, ref in enumerate((zr, zi)):
-        for g in range(2):
-            own = [ref[s, g * 8 : g * 8 + 8, :] for s in range(16)]
-            other = [ref[16 + s, g * 8 : g * 8 + 8, :] for s in range(16)]
-            values = [a + jnp.where(place > 0, b, 0.0) for a, b in zip(own, other)]
-            for a, value in enumerate(swap_bits(values, lane)):
-                out_ref[a, part * 16 + g * 8 : part * 16 + g * 8 + 8, :] = value
-            for q in range(2):
-                pack = other[8 * q]
-                for j in range(1, 8):
-                    pack = jnp.where(place == j, pltpu.roll(other[8 * q + j], j * slabs, 1), pack)
-                spill.append(pack)
-    turned = jnp.concatenate(spill + spill, axis=0).T
-    for j in range(8):
-        turn[j * 17 : j * 17 + 16, :] = turned[j * 16 : j * 16 + 16, :]
-    report = jnp.zeros((8, LANES), jnp.float32)
-    for step, total in enumerate(totals):
-        report = jnp.where((sub == step) & (lane == 64 + tile), total, report)
-    for a in range(16):
-        out_ref[a, 32:40, :] = jnp.where(lane < 64, turn[pl.ds(a, 8, stride=17), :], report)
-
-
-def filter_tiles(slabs, blocks, tiles, packed, data):
-    shape = (16, 40, LANES) if packed else (33, 16, LANES)
-    body = functools.partial(filter_kernel, slabs, blocks, tiles, packed)
+        for s in range(16):
+            out_ref[part * 16 + s, :, :] = ref[s, 0:16, :]
+
+
+def filter_tiles(slabs, blocks, tiles, data):
+    body = functools.partial(filter_kernel, slabs, blocks, tiles)
     return pl.pallas_call(
         body,
-        out_shape=jax.ShapeDtypeStruct(shape, jnp.float32),
+        out_shape=jax.ShapeDtypeStruct((33, 16, LANES), jnp.float32),
         in_specs=[pl.BlockSpec(memory_space=pltpu.VMEM)],
         out_specs=pl.BlockSpec(memory_space=pltpu.VMEM),
         scratch_shapes=[pltpu.VMEM((tiles * 16, 24, LANES), jnp.float32)] * 2
@@ -368,9 +345,276 @@
         + [pltpu.VMEM((136, LANES), jnp.float32)] * 4
         + [pltpu.VMEM((tiles * 4 * 144, LANES), jnp.float32)] * 2
         + [pltpu.VMEM((144, LANES), jnp.float32)] * 4
-        + [pltpu.VMEM((rows, LANES), jnp.float32) for rows in (tiles * 16, tiles * 32, ITERS * 16, 136)],
+        + [pltpu.VMEM((rows, LANES), jnp.float32) for rows in (tiles * 16, tiles * 32, ITERS * 16)],
         compiler_params=pltpu.CompilerParams(vmem_limit_bytes=16 << 20),
         name="filter_tiles",
+    )(data)
+
+
+def column_kernel(in_ref, out_ref, *scratch):
+    zr, zi, yr, yi, wr, wi, shift_r, shift_i, gain, turn = scratch[:10]
+    buffers = [scratch[10 + 6 * k : 16 + 6 * k] for k in range(2)]
+    final = scratch[22:25]
+    tile = lax.axis_index("rows")
+    lane = lax.broadcasted_iota(jnp.int32, (8, LANES), 1)
+    sub = lax.broadcasted_iota(jnp.int32, (8, LANES), 0)
+    in_slab = lane & 7
+
+    def inside(first):
+        column = tile * 8 + (first - 2) + sub
+        return jnp.where((column >= 0) & (column < 128), 1.0, 0.0)
+
+    def block(body):
+        pl.when(tile >= 0)(body)
+
+    def run(count, body):
+        lax.fori_loop(0, count, lambda i, c: (body(i), c)[1], 0)
+
+    zero = jnp.zeros((8, LANES), jnp.float32)
+    for vr, vi, pr, pi, qr, qi in buffers:
+        for ref in (vr, vi):
+            for row in (272, 280, 288):
+                ref[row : row + 8, :] = zero
+        for ref in (qr, qi):
+            for t in range(16):
+                ref[t * 17 : t * 17 + 1, :] = zero[0:1]
+
+    for g in range(2):
+        for h in range(2):
+            stacked = jnp.concatenate([in_ref[a, h * 16 + g * 8 : h * 16 + g * 8 + 8, :] for a in range(16)], axis=0)
+            base = (g * 2 + h) * 136
+            turned = stacked.T
+            for b in range(8):
+                turn[base + b * 17 : base + b * 17 + 16, :] = turned[b * 16 : b * 16 + 16]
+    halo = jnp.where(sub < 3, inside(10), jnp.where(sub > 5, inside(-6), 0.0))
+    for g in range(2):
+        for h, mask in enumerate((None, halo)):
+            for s in range(16):
+                value = cos_sin(turn[pl.ds((g * 2 + h) * 136 + s, 8, stride=17), :])
+                for ref, v in zip((zr, zi), value):
+                    if h == 0:
+                        ref[g * 16 + s, 2:10, :] = v
+                    else:
+                        ref[g * 16 + s, 10:13, :] = (v * mask)[0:3]
+                        ref[g * 16 + s, 0:2, :] = (v * mask)[6:8]
+
+    def forward_columns(first, width, g):
+        energies = []
+        for j in range(-(-width // 8)):
+            rows = min(8, width - 8 * j)
+            at = first + 8 * j
+            near = [(zr[g * 16 + s, at : at + 8, :], zi[g * 16 + s, at : at + 8, :]) for s in range(16)]
+            far = [(zr[g * 16 + s, at + 1 : at + 9, :], zi[g * 16 + s, at + 1 : at + 9, :]) for s in range(16)]
+            power = zero
+            for a, b in zip(near, far):
+                power = power + ((a[0] * a[0] + a[1] * a[1]) + (b[0] * b[0] + b[1] * b[1]))
+            energies.append(power)
+            even = fft([plus(a, b) for a, b in zip(near, far)], -1)
+            odd = odd_outputs([minus(a, b) for a, b in zip(near, far)])
+            for l in range(32):
+                re, im = (even, odd)[l % 2][l // 2]
+                to = pl.ds(g * 400 + l * width + 8 * j, rows)
+                yr[to, :] = re[0:rows]
+                yi[to, :] = im[0:rows]
+        for j, power in enumerate(energies):
+            gain[pl.ds(pl.multiple_of(48 + g * 16 + j * 8, 8), 8), :] = power
+
+    def turn_in(chunk):
+        vr, vi = buffers[chunk % 2][:2]
+        for source, ref in ((yr, vr), (yi, vi)):
+            for g in range(2):
+                turned = source[g * 400 + chunk * 128 : g * 400 + chunk * 128 + 128, :].T
+                for a in range(16):
+                    ref[a * 17 + g * 8 : a * 17 + g * 8 + 8, :] = turned[a * 8 : a * 8 + 8]
+
+    def turn_out(chunk):
+        pr, pi, qr, qi = buffers[chunk % 2][2:]
+        for p, q, target in ((pr, qr, wr), (pi, qi, wi)):
+            for g in range(2):
+                parts = []
+                for a in range(16):
+                    at = pl.ds(g * 136 + a, 8, stride=17)
+                    parts.append(p[at, :] + q[at, :])
+                target[g * 400 + chunk * 128 : g * 400 + chunk * 128 + 128, :] = jnp.concatenate(parts, axis=0).T
+
+    def window_gains(width, chunks):
+        power = [gain[48 + j * 8 : 56 + j * 8, :] + gain[64 + j * 8 : 72 + j * 8, :] for j in range(2)]
+        power[1] = jnp.where(sub < width - 8, power[1], 0.0)
+        row = lax.broadcasted_iota(jnp.int32, (16, LANES), 0)
+        slab = lax.broadcasted_iota(jnp.int32, (16, LANES), 1) // 8
+        pick = jnp.where((slab == row) | (slab == row + 1), 1.0, 0.0)
+        exact = dict(precision=lax.Precision.HIGHEST, preferred_element_type=jnp.float32)
+        mean = lax.dot_general(pick, jnp.concatenate(power, axis=0), (((1,), (1,)), ((), ())), **exact)
+        column = lax.broadcasted_iota(jnp.int32, (16, chunks * 128), 1)
+        column = column - width * ((column.astype(jnp.float32) + 0.5) * (1.0 / width)).astype(jnp.int32)
+        spread = jnp.where(column == lax.broadcasted_iota(jnp.int32, (16, chunks * 128), 0), 1.0, 0.0)
+        value = lax.dot_general(1.0 / (mean + EPS), spread, (((1,), (0,)), ((), ())), **exact)
+        for c in range(chunks):
+            gain[c * 16 : c * 16 + 16, :] = value[:, c * 128 : c * 128 + 128]
+
+    def residues():
+        def corner(s):
+            at = 2 if s < 16 else 3
+            result = []
+            for ref in (zr, zi):
+                top = ref[s % 16, at : at + 8, :]
+                low = ref[16 + s % 16, at : at + 8, :]
+                top_left = pltpu.roll(top, LANES - 1, 1)
+                low_left = pltpu.roll(low, LANES - 1, 1)
+                top_under = jnp.where(in_slab < 7, top_left, pltpu.roll(low, 7, 1))
+                low_under = jnp.where(in_slab < 7, low_left, jnp.where(lane < LANES - 1, top_left, 0.0))
+                result.append((top, low, top_under, low_under))
+            return [((result[0][g], result[1][g]), (result[0][2 + g], result[1][2 + g])) for g in range(2)]
+
+        def cross(a, b):
+            return a[1] * b[0] - a[0] * b[1]
+
+        total = zero
+        here = corner(0)
+        down = [cross(*pair) for pair in here]
+        for s in range(16):
+            following = corner(s + 1)
+            following_down = [cross(*pair) for pair in following]
+            for g in range(2):
+                across = cross(here[g][0], following[g][0]) - cross(here[g][1], following[g][1])
+                loop = across + (following_down[g] - down[g])
+                total = total + loop * loop
+            here, down = following, following_down
+        return total
+
+    def windows(chunk, half):
+        vr, vi, pr, pi, qr, qi = buffers[chunk % 2]
+        scale = gain[chunk * 16 + half * 8 : chunk * 16 + half * 8 + 8, :]
+        sums = []
+        differences = []
+        for t in range(16):
+            at = pl.ds(half * 136 + t, 8, stride=17)
+            after = pl.ds(half * 136 + 17 + t, 8, stride=17)
+            near = (vr[at, :], vi[at, :])
+            far = (vr[after, :], vi[after, :])
+            sums.append(plus(near, far))
+            differences.append(minus(near, far))
+        back = []
+        for spectrum in (lambda: fft(sums, -1), lambda: odd_outputs(differences)):
+            filtered = []
+            for re, im in spectrum():
+                factor = lax.rsqrt(lax.rsqrt((re * re + im * im) * scale))
+                filtered.append((re * factor, im * factor))
+            back.append(filtered)
+        back = fft(back[0], 1), join(fft(back[1][0::2], 1), fft(back[1][1::2], 1), 32, 1)
+        for t in range(16):
+            upper = plus(back[0][t], back[1][t])
+            lower = minus(back[0][t], back[1][t])
+            at = pl.ds(t * 17 + half * 8, 8)
+            pr[at, :], pi[at, :] = (v * (ramp(t) / 32) for v in upper)
+            at = pl.ds(t * 17 + half * 8 + 1, 8)
+            qr[at, :], qi[at, :] = (v * (ramp(t + 16) / 32) for v in lower)
+
+    def inverse_columns(first, width, last, g):
+        groups = range(-(-width // 8))
+        kept = []
+        for j in groups:
+            here = inside(first + 8 * j)
+            both = here * inside(first + 8 * j + 1)
+            values = []
+            for l in range(32):
+                at = pl.ds(g * 400 + l * width + 8 * j, 8)
+                values.append((wr[at, :], wi[at, :]))
+            even = fft(values[0::2], 1)
+            odd = join(fft(values[1::4], 1), fft(values[3::4], 1), 32, 1)
+            for s in range(16):
+                weight = here * (ramp(s) / 32)
+                own = [v * weight for v in plus(even[s], odd[s])]
+                weight = both * (ramp(s + 16) / 32)
+                other = [v * weight for v in minus(even[s], odd[s])]
+                if last:
+                    for part in range(2):
+                        base = (part * 2 + g) * 144 + s * 9
+                        final[0][pl.ds(base, 8), :] = own[part]
+                        final[1][pl.ds(base + 1, 8), :] = other[part]
+                else:
+                    kept.append(own)
+                    shift_r[s * 24 + 8 * j + 1 : s * 24 + 8 * j + 9, :] = other[0]
+                    shift_i[s * 24 + 8 * j + 1 : s * 24 + 8 * j + 9, :] = other[1]
+        if last:
+            return
+        for j in groups:
+            rows = min(8, width - 8 * j)
+            for s in range(16):
+                for part, (ref, shift) in enumerate(((zr, shift_r), (zi, shift_i))):
+                    value = kept[j * 16 + s][part] + shift[s * 24 + 8 * j : s * 24 + 8 * j + 8, :]
+                    ref[g * 16 + s, first + 8 * j : first + 8 * j + rows, :] = value[0:rows]
+
+    for k in range(4):
+        for s in range(16):
+            final[1][k * 144 + s * 9 : k * 144 + s * 9 + 1, :] = zero[0:1]
+
+    for step in range(ITERS):
+        first = step
+        width = 12 - 2 * step
+        chunks = -(-width // 4)
+        last = step == ITERS - 1
+        run(2, functools.partial(forward_columns, first, width))
+
+        @block
+        def _():
+            window_gains(width, chunks)
+            turn_in(0)
+            final[2][step * 8 : step * 8 + 8, :] = residues()
+
+        for chunk in range(chunks):
+
+            @block
+            def _():
+                if chunk + 1 < chunks:
+                    turn_in(chunk + 1)
+                windows(chunk, 0)
+                windows(chunk, 1)
+                if chunk:
+                    turn_out(chunk - 1)
+
+        block(lambda: turn_out(chunks - 1))
+        run(2, functools.partial(inverse_columns, first, width, last))
+
+    spill = []
+    for part in range(2):
+        for g in range(2):
+            base = (part * 2 + g) * 144
+            rows = []
+            for b in range(8):
+                for s in (0, 8):
+                    at = pl.ds(base + s * 9 + b, 8, stride=9)
+                    rows.append(final[0][at, :] + final[1][at, :])
+            turned = jnp.concatenate(rows, axis=0).T
+            for a in range(16):
+                out_ref[a, part * 16 + g * 8 : part * 16 + g * 8 + 8, :] = turned[a * 8 : a * 8 + 8]
+            spill += [final[1][pl.ds(base + s * 9 + 8, 8, stride=9), :] for s in (0, 8)]
+    turned = jnp.concatenate(spill + spill, axis=0).T
+    report = zero
+    for step in range(ITERS):
+        total = jnp.sum(final[2][step * 8 : step * 8 + 8, :])
+        report = jnp.where((sub == step) & (lane == 64 + tile), total, report)
+    for a in range(16):
+        out_ref[a, 32:40, :] = jnp.where(lane < 64, turned[a * 8 : a * 8 + 8], report)
+
+
+def filter_columns(data):
+    def rows(count):
+        return pltpu.VMEM((count, LANES), jnp.float32)
+
+    return pl.pallas_call(
+        column_kernel,
+        out_shape=jax.ShapeDtypeStruct((16, 40, LANES), jnp.float32),
+        in_specs=[pl.BlockSpec(memory_space=pltpu.VMEM)],
+        out_specs=pl.BlockSpec(memory_space=pltpu.VMEM),
+        scratch_shapes=[pltpu.VMEM((32, 24, LANES), jnp.float32)] * 2
+        + [rows(800)] * 4
+        + [rows(384)] * 2
+        + [rows(80), rows(544)]
+        + ([rows(296)] * 2 + [rows(280)] * 4) * 2
+        + [rows(584), rows(584), rows(ITERS * 8)],
+        compiler_params=pltpu.CompilerParams(vmem_limit_bytes=16 << 20),
+        name="filter_columns",
     )(data)
 
 
@@ -379,18 +623,13 @@
     extras = [in_ref[c, 32:40, :] for c in range(16)]
     sums = functools.reduce(jnp.add, extras)
     profile_ref[...] = pltpu.roll(sums, 64, 1)[:ITERS, :16] * scale
-    turned = jnp.concatenate(extras, axis=0).T
-    low = (lane & 8) == 0
     for part in range(2):
         for g in range(2):
-            first = (part * 2 + g) * 16
-            a = turned[first : first + 8]
-            b = turned[first + 8 : first + 16]
-            pairs = (jnp.where(low, a, pltpu.roll(b, 8, 1)), jnp.where(low, pltpu.roll(a, LANES - 8, 1), b))
+            offset = (part * 2 + g) * 16
             for c in range(16):
                 value = in_ref[c, part * 16 + g * 8 : part * 16 + g * 8 + 8, :]
                 if c:
-                    spill = pltpu.roll(pairs[(c - 1) % 2], (LANES - (c - 1) // 2 * 16) % LANES, 1)
+                    spill = pltpu.roll(extras[c - 1], LANES - offset, 1) if offset else extras[c - 1]
                     value = value + jnp.where(lane < 16, spill, 0.0)
                 field_ref[part, g * 8 : g * 8 + 8, c * LANES : (c + 1) * LANES] = value
 
@@ -433,7 +672,6 @@
         raise ValueError("unsupported sizes")
     scale = 1.0 / (height * devices * 128.0)
     if devices == 16:
-        tiles = 2
         columns = phase.reshape(16, devices, LANES).transpose(1, 0, 2)
         empty = jnp.zeros((1, 16, LANES), phase.dtype)
         after = jnp.concatenate([columns[1:], empty])
@@ -441,13 +679,13 @@
         lane = lax.broadcasted_iota(jnp.int32, columns.shape, 2)
         data = jnp.concatenate([columns, jnp.where(lane < LANES // 2, after, before)], axis=1)
         data = lax.all_to_all(data, "rows", 0, 0)
-        result = filter_tiles(devices, blocks, tiles, True, data)
+        result = filter_columns(data)
         result = lax.all_to_all(result, "rows", 0, 0)
         return finish(scale, result)
     tiles = -(-(blocks + 2 * HALO) // per_tile)
     data = lax.all_to_all(ring_of_blocks(phase, devices, blocks, tiles), "rows", 0, 0)
     data = data.reshape(devices, 16, tiles, per_tile, 16).transpose(2, 4, 1, 3, 0)
-    result = filter_tiles(devices, blocks, tiles, False, data.reshape(tiles, 16, 16, LANES))
+    result = filter_tiles(devices, blocks, tiles, data.reshape(tiles, 16, 16, LANES))
     field = result[:32].reshape(2, 16, 16, per_tile, devices).transpose(4, 0, 2, 3, 1)
     field = field.reshape(devices, 32, per_tile * 16)
     sums = jnp.broadcast_to(result[32, :ITERS, : per_tile * 16][None], (devices, ITERS, per_tile * 16))

time: 42.4 us -> 40.4 us (0.953)
  Pallas kernels: 9.6 us -> 7.55 us
    pallas_call x1, Pallas kernels: 8.62 us -> 6.72 us  [filter_columns(): pl.pallas_call(column_kernel, out_shape=jax.ShapeDtypeStruct((16, 40, LAN...]
where the time goes in v3:
time: 40.4 us; the launch traced here: 40.2 us
  blocking collectives  31 us (77%)
  Pallas kernels  7.55 us (19%)
  local copies, waits for them, and re-layouts  0.92 us (2%)
  between operations  0.66 us (2%)
    all_to_all x1, blocking collectives, per_device(): data = lax.all_to_all(data, 'rows', 0, 0)  17.2 us
    all_to_all x1, blocking collectives, per_device(): result = lax.all_to_all(result, 'rows', 0, 0)  13.7 us
    pallas_call x1, Pallas kernels, filter_columns(): pl.pallas_call(column_kernel, out_shape=jax.ShapeDtypeStruct((16, 40, LAN...  6.72 us
    unnamed x2, local copies, waits for them, and re-layouts  0.89 us
    pallas_call x1, Pallas kernels, finish(): pl.pallas_call(functools.partial(finish_kernel, scale), out_shape=(jax.Sh...  0.82 us

profile of v3, /device:TPU:0, one launch (start us, length us, event | category | flops | bytes accessed | tf_op | source)
XLA Modules:
  0.0 40.2 jit_solution(6703079334627036742)
XLA Ops:
  0.6 0.0 copy-start
  0.7 0.9 %copy-done = f32[16,2048]{1,0:T(8,128)S(1)} copy-done((f32[16,2048]{1,0:T(8,128)S(1)}, f32[16,2048]{1,0:T(8,128)}, u32[]{:S(2)}) %copy-start) | copy-done | bytes 131096
  1.6 17.2 %all_to_all.10.in_ref = f32[16,32,128]{2,1,0:T(8,128)S(1)} all-to-all(f32[16,32,128]{2,1,0:T(8,128)S(1)} %pad_maximum_fusion), channel_id=1, replica_groups=mesh['groups'=2,'rows'=16] {'rows'}, dimensions={0} | all-to-all | bytes 524288 | tf_op jit(solution)/shard_map/all_to_all | solution.py:681
  18.9 6.7 %filter_columns.1 = f32[16,40,128]{2,1,0:T(8,128)S(1)} custom-call(f32[16,32,128]{2,1,0:T(8,128)S(1)} %all_to_all.10.in_ref), custom_call_target="tpu_custom_call" | custom-call | tf_op jit(solution)/shard_map/filter_columns/pallas_call | solution.py:605
  25.6 13.7 %all_to_all.11.in_ref = f32[16,40,128]{2,1,0:T(8,128)S(1)} all-to-all(f32[16,40,128]{2,1,0:T(8,128)S(1)} %filter_columns.1), channel_id=1, replica_groups=mesh['groups'=2,'rows'=16] {'rows'}, dimensions={0} | all-to-all | bytes 655360 | tf_op jit(solution)/shard_map/all_to_all | solution.py:683
  39.3 0.8 %finish.1 = (f32[2,16,2048]{2,1,0:T(8,128)}, f32[3,16]{1,0:T(4,128)}) custom-call(f32[16,40,128]{2,1,0:T(8,128)S(1)} %all_to_all.11.in_ref), custom_call_target="tpu_custom_call" | custom-call | tf_op jit(solution)/shard_map/finish/pallas_call | solution.py:638
  (5 shorter events, 0.1 us)
Async XLA Ops:
  0.6 0.9 %copy-start = (f32[16,2048]{1,0:T(8,128)S(1)}, f32[16,2048]{1,0:T(8,128)}, u32[]{:S(2)}) copy-start(f32[16,2048]{1,0:T(8,128)} %param.1) | copy-start | bytes 393220

commit v4 on v3

--- a/solution.py
+++ b/solution.py
@@ -11,6 +11,8 @@
 ITERS = 3
 EPS = 1e-06
 LANES = 128
+IN_ROWS = 26
+OUT_ROWS = 37
 HALO = 3
 
 SIN = (9.99999996e-01, -1.66666580e-01, 8.33305053e-03, -1.98090400e-04, 2.60515161e-06)
@@ -351,6 +353,41 @@
     )(data)
 
 
+def pack_kernel(in_ref, out_ref, turn):
+    lane = lax.broadcasted_iota(jnp.int32, (8, LANES), 1)
+    zero = jnp.zeros((8, LANES), jnp.float32)
+    columns = [[in_ref[g * 8 : g * 8 + 8, c * LANES : (c + 1) * LANES] for g in range(2)] for c in range(16)]
+    for c in range(16):
+        after = columns[c + 1] if c < 15 else [zero, zero]
+        before = columns[c - 1] if c else [zero, zero]
+        at = c * IN_ROWS
+        out_ref[at : at + 8, :] = columns[c][0]
+        out_ref[at + 8 : at + 16, :] = columns[c][1]
+        first = jnp.where(lane < 32, after[0], pltpu.roll(before[0], 64, 1))
+        second = jnp.where(lane < 96, pltpu.roll(after[1], 64, 1), before[1])
+        out_ref[at + 16 : at + 24, :] = jnp.where(lane < 64, first, second)
+        turn[c * 8 : c * 8 + 8, :] = jnp.where(lane < 16, pltpu.roll(after[0], 96, 1), pltpu.roll(after[1], 112, 1))
+    for q in range(4):
+        rows = turn[pl.ds(q * 32, 8, stride=4), :]
+        for u in range(1, 4):
+            rows = jnp.where(lane // 32 == u, pltpu.roll(turn[pl.ds(q * 32 + u, 8, stride=4), :], 32 * u, 1), rows)
+        for k in range(4):
+            at = (q * 4 + k) * IN_ROWS + 24
+            out_ref[at : at + 2, :] = rows[k * 2 : k * 2 + 2]
+
+
+def pack(phase):
+    return pl.pallas_call(
+        pack_kernel,
+        out_shape=jax.ShapeDtypeStruct((16 * IN_ROWS, LANES), jnp.float32),
+        in_specs=[pl.BlockSpec(memory_space=pltpu.VMEM)],
+        out_specs=pl.BlockSpec(memory_space=pltpu.VMEM),
+        scratch_shapes=[pltpu.VMEM((128, LANES), jnp.float32)],
+        compiler_params=pltpu.CompilerParams(vmem_limit_bytes=8 << 20),
+        name="pack",
+    )(phase)
+
+
 def column_kernel(in_ref, out_ref, *scratch):
     zr, zi, yr, yi, wr, wi, shift_r, shift_i, gain, turn = scratch[:10]
     buffers = [scratch[10 + 6 * k : 16 + 6 * k] for k in range(2)]
@@ -379,24 +416,37 @@
             for t in range(16):
                 ref[t * 17 : t * 17 + 1, :] = zero[0:1]
 
+    def stacked(offset):
+        return jnp.concatenate([in_ref[a * IN_ROWS + offset : a * IN_ROWS + offset + 8, :] for a in range(16)], axis=0)
+
+    for k, offset in enumerate((0, 8, 16)):
+        turned = stacked(offset).T
+        for b in range(8):
+            turn[k * 136 + b * 17 : k * 136 + b * 17 + 16, :] = turned[b * 16 : b * 16 + 16]
+    tail = jnp.concatenate([in_ref[a * IN_ROWS + 24 : a * IN_ROWS + 26, :] for a in range(16)], axis=0)
+    for q in range(4):
+        for u in range(4):
+            value = tail[q * 8 : q * 8 + 8]
+            turn[pl.ds(408 + q * 32 + u, 8, stride=4), :] = pltpu.roll(value, LANES - 32 * u, 1) if u else value
+    turned = turn[408:536, :].T[0:32]
+    beyond = jnp.where(tile * 8 + 10 < 128, 1.0, 0.0)
+    for ref, v in zip((zr, zi), cos_sin(turned)):
+        for k in range(32):
+            ref[k, 12:13, :] = v[k : k + 1] * beyond
     for g in range(2):
-        for h in range(2):
-            stacked = jnp.concatenate([in_ref[a, h * 16 + g * 8 : h * 16 + g * 8 + 8, :] for a in range(16)], axis=0)
-            base = (g * 2 + h) * 136
-            turned = stacked.T
-            for b in range(8):
-                turn[base + b * 17 : base + b * 17 + 16, :] = turned[b * 16 : b * 16 + 16]
-    halo = jnp.where(sub < 3, inside(10), jnp.where(sub > 5, inside(-6), 0.0))
-    for g in range(2):
-        for h, mask in enumerate((None, halo)):
-            for s in range(16):
-                value = cos_sin(turn[pl.ds((g * 2 + h) * 136 + s, 8, stride=17), :])
-                for ref, v in zip((zr, zi), value):
-                    if h == 0:
-                        ref[g * 16 + s, 2:10, :] = v
-                    else:
-                        ref[g * 16 + s, 10:13, :] = (v * mask)[0:3]
-                        ref[g * 16 + s, 0:2, :] = (v * mask)[6:8]
+        for s in range(16):
+            value = cos_sin(turn[pl.ds(g * 136 + s, 8, stride=17), :])
+            for ref, v in zip((zr, zi), value):
+                ref[g * 16 + s, 2:10, :] = v
+    edge = tile * 8 + jnp.where((sub & 3) < 2, 8 + (sub & 3), (sub & 3) - 4)
+    edge = jnp.where((edge >= 0) & (edge < 128), 1.0, 0.0)
+    for s in range(16):
+        value = cos_sin(turn[pl.ds(272 + s, 8, stride=17), :])
+        for ref, v in zip((zr, zi), value):
+            v = v * edge
+            for g in range(2):
+                ref[g * 16 + s, 10:12, :] = v[g * 4 : g * 4 + 2]
+                ref[g * 16 + s, 0:2, :] = v[g * 4 + 2 : g * 4 + 4]
 
     def forward_columns(first, width, g):
         energies = []
@@ -587,15 +637,18 @@
                     rows.append(final[0][at, :] + final[1][at, :])
             turned = jnp.concatenate(rows, axis=0).T
             for a in range(16):
-                out_ref[a, part * 16 + g * 8 : part * 16 + g * 8 + 8, :] = turned[a * 8 : a * 8 + 8]
+                at = a * OUT_ROWS + part * 16 + g * 8
+                out_ref[at : at + 8, :] = turned[a * 8 : a * 8 + 8]
             spill += [final[1][pl.ds(base + s * 9 + 8, 8, stride=9), :] for s in (0, 8)]
     turned = jnp.concatenate(spill + spill, axis=0).T
-    report = zero
+    report = zero[0:1]
     for step in range(ITERS):
         total = jnp.sum(final[2][step * 8 : step * 8 + 8, :])
-        report = jnp.where((sub == step) & (lane == 64 + tile), total, report)
+        report = jnp.where(lane[0:1] == step * 16 + tile, total, report)
     for a in range(16):
-        out_ref[a, 32:40, :] = jnp.where(lane < 64, turned[a * 8 : a * 8 + 8], report)
+        value = turned[a * 8 : a * 8 + 8]
+        out_ref[a * OUT_ROWS + 32 : a * OUT_ROWS + 36, :] = jnp.where(lane[0:4] < 64, value[0:4], value[4:8])
+        out_ref[a * OUT_ROWS + 36 : a * OUT_ROWS + 37, :] = report
 
 
 def filter_columns(data):
@@ -604,7 +657,7 @@
 
     return pl.pallas_call(
         column_kernel,
-        out_shape=jax.ShapeDtypeStruct((16, 40, LANES), jnp.float32),
+        out_shape=jax.ShapeDtypeStruct((16 * OUT_ROWS, LANES), jnp.float32),
         in_specs=[pl.BlockSpec(memory_space=pltpu.VMEM)],
         out_specs=pl.BlockSpec(memory_space=pltpu.VMEM),
         scratch_shapes=[pltpu.VMEM((32, 24, LANES), jnp.float32)] * 2
@@ -620,14 +673,20 @@
 
 def finish_kernel(scale, in_ref, field_ref, profile_ref):
     lane = lax.broadcasted_iota(jnp.int32, (8, LANES), 1)
-    extras = [in_ref[c, 32:40, :] for c in range(16)]
-    sums = functools.reduce(jnp.add, extras)
-    profile_ref[...] = pltpu.roll(sums, 64, 1)[:ITERS, :16] * scale
+    extras = []
+    sums = jnp.zeros((1, LANES), jnp.float32)
+    for c in range(16):
+        half = in_ref[c * OUT_ROWS + 32 : c * OUT_ROWS + 36, :]
+        extras.append(jnp.concatenate([half, pltpu.roll(half, 64, 1)], axis=0))
+        sums = sums + in_ref[c * OUT_ROWS + 36 : c * OUT_ROWS + 37, :]
+    for step in range(ITERS):
+        profile_ref[step : step + 1, :] = sums[:, step * 16 : step * 16 + 16] * scale
     for part in range(2):
         for g in range(2):
             offset = (part * 2 + g) * 16
             for c in range(16):
-                value = in_ref[c, part * 16 + g * 8 : part * 16 + g * 8 + 8, :]
+                at = c * OUT_ROWS + part * 16 + g * 8
+                value = in_ref[at : at + 8, :]
                 if c:
                     spill = pltpu.roll(extras[c - 1], LANES - offset, 1) if offset else extras[c - 1]
                     value = value + jnp.where(lane < 16, spill, 0.0)
@@ -672,15 +731,10 @@
         raise ValueError("unsupported sizes")
     scale = 1.0 / (height * devices * 128.0)
     if devices == 16:
-        columns = phase.reshape(16, devices, LANES).transpose(1, 0, 2)
-        empty = jnp.zeros((1, 16, LANES), phase.dtype)
-        after = jnp.concatenate([columns[1:], empty])
-        before = jnp.concatenate([empty, columns[:-1]])
-        lane = lax.broadcasted_iota(jnp.int32, columns.shape, 2)
-        data = jnp.concatenate([columns, jnp.where(lane < LANES // 2, after, before)], axis=1)
-        data = lax.all_to_all(data, "rows", 0, 0)
-        result = filter_columns(data)
-        result = lax.all_to_all(result, "rows", 0, 0)
+        data = lax.all_to_all(pack(phase).reshape(16, IN_ROWS, 1, LANES), "rows", 0, 0)
+        result = filter_columns(data.reshape(16 * IN_ROWS, LANES))
+        result = lax.all_to_all(result.reshape(16, OUT_ROWS, 1, LANES), "rows", 0, 0)
+        result = result.reshape(16 * OUT_ROWS, LANES)
         return finish(scale, result)
     tiles = -(-(blocks + 2 * HALO) // per_tile)
     data = lax.all_to_all(ring_of_blocks(phase, devices, blocks, tiles), "rows", 0, 0)

time: 40.4 us -> 39.3 us (0.973)
  blocking collectives: 31 us -> 29.7 us
    all_to_all x2, blocking collectives: 31 us -> 29.7 us  [the longest x1 16.4 us: per_device(): lax.all_to_all(pack(phase).reshape(16, IN_ROWS, 1, LANES), 'rows', 0, 0)]
    pallas_call x1 -> x2, Pallas kernels: 6.72 us -> 6.91 us  [the longest x1 6.72 us: filter_columns(): pl.pallas_call(column_kernel, out_shape=jax.ShapeDtypeStruct((16 * OUT_RO...]
where the time goes in v4:
time: 39.3 us; the launch traced here: 39 us
  blocking collectives  29.7 us (76%)
  Pallas kernels  7.8 us (20%)
  local copies, waits for them, and re-layouts  0.9 us (2%)
  between operations  0.64 us (2%)
    all_to_all x1, blocking collectives, per_device(): lax.all_to_all(pack(phase).reshape(16, IN_ROWS, 1, LANES), 'rows', 0, 0)  16.4 us
    all_to_all x1, blocking collectives, per_device(): lax.all_to_all(result.reshape(16, OUT_ROWS, 1, LANES), 'rows', 0, 0)  13.3 us
    pallas_call x1, Pallas kernels, filter_columns(): pl.pallas_call(column_kernel, out_shape=jax.ShapeDtypeStruct((16 * OUT_RO...  6.72 us
    unnamed x2, local copies, waits for them, and re-layouts  0.9 us
    pallas_call x1, Pallas kernels, finish(): pl.pallas_call(functools.partial(finish_kernel, scale), out_shape=(jax.Sh...  0.89 us

profile of v4, /device:TPU:0, one launch (start us, length us, event | category | flops | bytes accessed | tf_op | source)
XLA Modules:
  0.0 39.0 jit_solution(15514883341340056401)
XLA Ops:
  0.6 0.0 copy-start
  0.6 0.9 %copy-done = f32[16,2048]{1,0:T(8,128)S(1)} copy-done((f32[16,2048]{1,0:T(8,128)S(1)}, f32[16,2048]{1,0:T(8,128)}, u32[]{:S(2)}) %copy-start) | copy-done | bytes 131096
  1.5 0.2 pack.1
  1.7 16.4 %all_to_all.10 = f32[16,26,1,128]{3,2,1,0:T(1,128)S(1)} all-to-all(f32[16,26,1,128]{3,2,1,0:T(1,128)S(1)} %bitcast.7), channel_id=1, replica_groups=mesh['groups'=2,'rows'=16] {'rows'}, dimensions={0} | all-to-all | bytes 425984 | tf_op jit(solution)/shard_map/all_to_all | solution.py:734
  18.2 6.7 %filter_columns.1 = f32[592,128]{1,0:T(8,128)S(1)} custom-call(f32[416,128]{1,0:T(8,128)S(1)} %bitcast.6), custom_call_target="tpu_custom_call" | custom-call | tf_op jit(solution)/shard_map/filter_columns/pallas_call | solution.py:658
  24.9 13.3 %all_to_all.11 = f32[16,37,1,128]{3,2,1,0:T(1,128)S(1)} all-to-all(f32[16,37,1,128]{3,2,1,0:T(1,128)S(1)} %bitcast.5), channel_id=1, replica_groups=mesh['groups'=2,'rows'=16] {'rows'}, dimensions={0} | all-to-all | bytes 606208 | tf_op jit(solution)/shard_map/all_to_all | solution.py:736
  38.2 0.9 %finish.1 = (f32[2,16,2048]{2,1,0:T(8,128)}, f32[3,16]{1,0:T(4,128)}) custom-call(f32[592,128]{1,0:T(8,128)S(1)} %bitcast.4), custom_call_target="tpu_custom_call" | custom-call | tf_op jit(solution)/shard_map/finish/pallas_call | solution.py:697
Async XLA Ops:
  0.6 0.9 %copy-start = (f32[16,2048]{1,0:T(8,128)S(1)}, f32[16,2048]{1,0:T(8,128)}, u32[]{:S(2)}) copy-start(f32[16,2048]{1,0:T(8,128)} %in_ref.1) | copy-start | bytes 393220

commit v5 on v4

--- a/solution.py
+++ b/solution.py
@@ -13,6 +13,7 @@
 LANES = 128
 IN_ROWS = 26
 OUT_ROWS = 37
+PITCH = 40
 HALO = 3
 
 SIN = (9.99999996e-01, -1.66666580e-01, 8.33305053e-03, -1.98090400e-04, 2.60515161e-06)
@@ -398,7 +399,7 @@
     in_slab = lane & 7
 
     def inside(first):
-        column = tile * 8 + (first - 2) + sub
+        column = tile * 8 + (first - 2) + sub // 2
         return jnp.where((column >= 0) & (column < 128), 1.0, 0.0)
 
     def block(body):
@@ -432,12 +433,13 @@
     beyond = jnp.where(tile * 8 + 10 < 128, 1.0, 0.0)
     for ref, v in zip((zr, zi), cos_sin(turned)):
         for k in range(32):
-            ref[k, 12:13, :] = v[k : k + 1] * beyond
+            at = (k % 16) * PITCH + 24 + k // 16
+            ref[at : at + 1, :] = v[k : k + 1] * beyond
     for g in range(2):
         for s in range(16):
             value = cos_sin(turn[pl.ds(g * 136 + s, 8, stride=17), :])
             for ref, v in zip((zr, zi), value):
-                ref[g * 16 + s, 2:10, :] = v
+                ref[pl.ds(s * PITCH + 4 + g, 8, stride=2), :] = v
     edge = tile * 8 + jnp.where((sub & 3) < 2, 8 + (sub & 3), (sub & 3) - 4)
     edge = jnp.where((edge >= 0) & (edge < 128), 1.0, 0.0)
     for s in range(16):
@@ -445,35 +447,34 @@
         for ref, v in zip((zr, zi), value):
             v = v * edge
             for g in range(2):
-                ref[g * 16 + s, 10:12, :] = v[g * 4 : g * 4 + 2]
-                ref[g * 16 + s, 0:2, :] = v[g * 4 + 2 : g * 4 + 4]
-
-    def forward_columns(first, width, g):
-        energies = []
-        for j in range(-(-width // 8)):
-            rows = min(8, width - 8 * j)
-            at = first + 8 * j
-            near = [(zr[g * 16 + s, at : at + 8, :], zi[g * 16 + s, at : at + 8, :]) for s in range(16)]
-            far = [(zr[g * 16 + s, at + 1 : at + 9, :], zi[g * 16 + s, at + 1 : at + 9, :]) for s in range(16)]
-            power = zero
-            for a, b in zip(near, far):
-                power = power + ((a[0] * a[0] + a[1] * a[1]) + (b[0] * b[0] + b[1] * b[1]))
-            energies.append(power)
-            even = fft([plus(a, b) for a, b in zip(near, far)], -1)
-            odd = odd_outputs([minus(a, b) for a, b in zip(near, far)])
-            for l in range(32):
-                re, im = (even, odd)[l % 2][l // 2]
-                to = pl.ds(g * 400 + l * width + 8 * j, rows)
-                yr[to, :] = re[0:rows]
-                yi[to, :] = im[0:rows]
-        for j, power in enumerate(energies):
-            gain[pl.ds(pl.multiple_of(48 + g * 16 + j * 8, 8), 8), :] = power
+                for k, place in enumerate((10, 11, 0, 1)):
+                    at = s * PITCH + 2 * place + g
+                    ref[at : at + 1, :] = v[g * 4 + k : g * 4 + k + 1]
+
+    def forward_columns(first, width, j):
+        near = []
+        far = []
+        power = zero
+        for s in range(16):
+            at = pl.ds(s * PITCH + 2 * first + j * 8, 8)
+            after = pl.ds(s * PITCH + 2 * first + 2 + j * 8, 8)
+            near.append((zr[at, :], zi[at, :]))
+            far.append((zr[after, :], zi[after, :]))
+            a, b = near[-1], far[-1]
+            power = power + ((a[0] * a[0] + a[1] * a[1]) + (b[0] * b[0] + b[1] * b[1]))
+        gain[pl.ds(pl.multiple_of(48 + j * 8, 8), 8), :] = power
+        even = fft([plus(a, b) for a, b in zip(near, far)], -1)
+        odd = odd_outputs([minus(a, b) for a, b in zip(near, far)])
+        for l in range(32):
+            to = pl.ds(l * 2 * width + j * 8, 8)
+            yr[to, :], yi[to, :] = (even, odd)[l % 2][l // 2]
 
     def turn_in(chunk):
         vr, vi = buffers[chunk % 2][:2]
         for source, ref in ((yr, vr), (yi, vi)):
             for g in range(2):
-                turned = source[g * 400 + chunk * 128 : g * 400 + chunk * 128 + 128, :].T
+                parts = [source[pl.ds(chunk * 256 + i * 16 + g, 8, stride=2), :] for i in range(16)]
+                turned = jnp.concatenate(parts, axis=0).T
                 for a in range(16):
                     ref[a * 17 + g * 8 : a * 17 + g * 8 + 8, :] = turned[a * 8 : a * 8 + 8]
 
@@ -485,30 +486,34 @@
                 for a in range(16):
                     at = pl.ds(g * 136 + a, 8, stride=17)
                     parts.append(p[at, :] + q[at, :])
-                target[g * 400 + chunk * 128 : g * 400 + chunk * 128 + 128, :] = jnp.concatenate(parts, axis=0).T
-
-    def window_gains(width, chunks):
-        power = [gain[48 + j * 8 : 56 + j * 8, :] + gain[64 + j * 8 : 72 + j * 8, :] for j in range(2)]
-        power[1] = jnp.where(sub < width - 8, power[1], 0.0)
+                turned = jnp.concatenate(parts, axis=0).T
+                for i in range(16):
+                    target[pl.ds(chunk * 256 + i * 16 + g, 8, stride=2), :] = turned[i * 8 : i * 8 + 8]
+
+    def window_gains(valid, width):
+        count = 2 * width
+        power = jnp.concatenate(
+            [jnp.where(sub < 2 * valid - 8 * j, gain[48 + j * 8 : 56 + j * 8, :], 0.0) for j in range(count // 8)], axis=0
+        )
         row = lax.broadcasted_iota(jnp.int32, (16, LANES), 0)
         slab = lax.broadcasted_iota(jnp.int32, (16, LANES), 1) // 8
         pick = jnp.where((slab == row) | (slab == row + 1), 1.0, 0.0)
         exact = dict(precision=lax.Precision.HIGHEST, preferred_element_type=jnp.float32)
-        mean = lax.dot_general(pick, jnp.concatenate(power, axis=0), (((1,), (1,)), ((), ())), **exact)
-        column = lax.broadcasted_iota(jnp.int32, (16, chunks * 128), 1)
+        mean = lax.dot_general(pick, power, (((1,), (1,)), ((), ())), **exact)
+        column = lax.broadcasted_iota(jnp.int32, (count, 32 * width), 1)
         column = column - width * ((column.astype(jnp.float32) + 0.5) * (1.0 / width)).astype(jnp.int32)
-        spread = jnp.where(column == lax.broadcasted_iota(jnp.int32, (16, chunks * 128), 0), 1.0, 0.0)
-        value = lax.dot_general(1.0 / (mean + EPS), spread, (((1,), (0,)), ((), ())), **exact)
-        for c in range(chunks):
-            gain[c * 16 : c * 16 + 16, :] = value[:, c * 128 : c * 128 + 128]
+        spread = jnp.where(column == lax.broadcasted_iota(jnp.int32, (count, 32 * width), 0) // 2, 1.0, 0.0)
+        mean = lax.dot_general(mean, spread, (((1,), (0,)), ((), ())), **exact)
+        for c in range(width // 4):
+            gain[c * 16 : c * 16 + 16, :] = 1.0 / (mean[:, c * 128 : c * 128 + 128] + EPS)
 
     def residues():
         def corner(s):
-            at = 2 if s < 16 else 3
+            at = s * PITCH + 4 if s < 16 else 6
             result = []
             for ref in (zr, zi):
-                top = ref[s % 16, at : at + 8, :]
-                low = ref[16 + s % 16, at : at + 8, :]
+                top = ref[pl.ds(at, 8, stride=2), :]
+                low = ref[pl.ds(at + 1, 8, stride=2), :]
                 top_left = pltpu.roll(top, LANES - 1, 1)
                 low_left = pltpu.roll(low, LANES - 1, 1)
                 top_under = jnp.where(in_slab < 7, top_left, pltpu.roll(low, 7, 1))
@@ -560,55 +565,44 @@
             at = pl.ds(t * 17 + half * 8 + 1, 8)
             qr[at, :], qi[at, :] = (v * (ramp(t + 16) / 32) for v in lower)
 
-    def inverse_columns(first, width, last, g):
-        groups = range(-(-width // 8))
-        kept = []
-        for j in groups:
-            here = inside(first + 8 * j)
-            both = here * inside(first + 8 * j + 1)
-            values = []
-            for l in range(32):
-                at = pl.ds(g * 400 + l * width + 8 * j, 8)
-                values.append((wr[at, :], wi[at, :]))
-            even = fft(values[0::2], 1)
-            odd = join(fft(values[1::4], 1), fft(values[3::4], 1), 32, 1)
-            for s in range(16):
-                weight = here * (ramp(s) / 32)
-                own = [v * weight for v in plus(even[s], odd[s])]
-                weight = both * (ramp(s + 16) / 32)
-                other = [v * weight for v in minus(even[s], odd[s])]
+    def inverse_columns(first, width, last, j):
+        here = inside(first + 4 * j)
+        both = here * inside(first + 4 * j + 1)
+        values = []
+        for l in range(32):
+            at = pl.ds(l * 2 * width + 8 * j, 8)
+            values.append((wr[at, :], wi[at, :]))
+        even = fft(values[0::2], 1)
+        odd = join(fft(values[1::4], 1), fft(values[3::4], 1), 32, 1)
+        for s in range(16):
+            weight = here * (ramp(s) / 32)
+            own = [v * weight for v in plus(even[s], odd[s])]
+            weight = both * (ramp(s + 16) / 32)
+            other = [v * weight for v in minus(even[s], odd[s])]
+            for part, (ref, shift) in enumerate(((zr, shift_r), (zi, shift_i))):
                 if last:
-                    for part in range(2):
-                        base = (part * 2 + g) * 144 + s * 9
-                        final[0][pl.ds(base, 8), :] = own[part]
-                        final[1][pl.ds(base + 1, 8), :] = other[part]
+                    base = part * 304 + s * 19 + 8 * j
+                    final[0][pl.ds(base, 8), :] = own[part]
+                    final[1][pl.ds(base + 2, 8), :] = other[part]
                 else:
-                    kept.append(own)
-                    shift_r[s * 24 + 8 * j + 1 : s * 24 + 8 * j + 9, :] = other[0]
-                    shift_i[s * 24 + 8 * j + 1 : s * 24 + 8 * j + 9, :] = other[1]
-        if last:
-            return
-        for j in groups:
-            rows = min(8, width - 8 * j)
-            for s in range(16):
-                for part, (ref, shift) in enumerate(((zr, shift_r), (zi, shift_i))):
-                    value = kept[j * 16 + s][part] + shift[s * 24 + 8 * j : s * 24 + 8 * j + 8, :]
-                    ref[g * 16 + s, first + 8 * j : first + 8 * j + rows, :] = value[0:rows]
-
-    for k in range(4):
-        for s in range(16):
-            final[1][k * 144 + s * 9 : k * 144 + s * 9 + 1, :] = zero[0:1]
+                    shift[pl.ds(s * 32 + 8 * j + 2, 8), :] = other[part]
+                    value = own[part] + shift[pl.ds(s * 32 + 8 * j, 8), :]
+                    ref[pl.ds(s * PITCH + 2 * first + 8 * j, 8), :] = value
+
+    for k in range(32):
+        final[1][k * 19 : k * 19 + 2, :] = zero[0:2]
 
     for step in range(ITERS):
         first = step
-        width = 12 - 2 * step
-        chunks = -(-width // 4)
+        valid = 12 - 2 * step
+        width = -(-valid // 4) * 4
+        chunks = width // 4
         last = step == ITERS - 1
-        run(2, functools.partial(forward_columns, first, width))
+        run(chunks, functools.partial(forward_columns, first, width))
 
         @block
         def _():
-            window_gains(width, chunks)
+            window_gains(valid, width)
             turn_in(0)
             final[2][step * 8 : step * 8 + 8, :] = residues()
 
@@ -624,22 +618,22 @@
                     turn_out(chunk - 1)
 
         block(lambda: turn_out(chunks - 1))
-        run(2, functools.partial(inverse_columns, first, width, last))
+        run(chunks, functools.partial(inverse_columns, first, width, last))
 
     spill = []
     for part in range(2):
         for g in range(2):
-            base = (part * 2 + g) * 144
+            base = part * 304 + g
             rows = []
             for b in range(8):
                 for s in (0, 8):
-                    at = pl.ds(base + s * 9 + b, 8, stride=9)
+                    at = pl.ds(base + s * 19 + 2 * b, 8, stride=19)
                     rows.append(final[0][at, :] + final[1][at, :])
             turned = jnp.concatenate(rows, axis=0).T
             for a in range(16):
                 at = a * OUT_ROWS + part * 16 + g * 8
                 out_ref[at : at + 8, :] = turned[a * 8 : a * 8 + 8]
-            spill += [final[1][pl.ds(base + s * 9 + 8, 8, stride=9), :] for s in (0, 8)]
+            spill += [final[1][pl.ds(base + s * 19 + 16, 8, stride=19), :] for s in (0, 8)]
     turned = jnp.concatenate(spill + spill, axis=0).T
     report = zero[0:1]
     for step in range(ITERS):
@@ -660,12 +654,12 @@
         out_shape=jax.ShapeDtypeStruct((16 * OUT_ROWS, LANES), jnp.float32),
         in_specs=[pl.BlockSpec(memory_space=pltpu.VMEM)],
         out_specs=pl.BlockSpec(memory_space=pltpu.VMEM),
-        scratch_shapes=[pltpu.VMEM((32, 24, LANES), jnp.float32)] * 2
-        + [rows(800)] * 4
-        + [rows(384)] * 2
+        scratch_shapes=[rows(16 * PITCH)] * 2
+        + [rows(776)] * 4
+        + [rows(520)] * 2
         + [rows(80), rows(544)]
         + ([rows(296)] * 2 + [rows(280)] * 4) * 2
-        + [rows(584), rows(584), rows(ITERS * 8)],
+        + [rows(624), rows(624), rows(ITERS * 8)],
         compiler_params=pltpu.CompilerParams(vmem_limit_bytes=16 << 20),
         name="filter_columns",
     )(data)

time: 39.3 us -> 39 us (level)
  no operation moved by 1% of the time
where the time goes in v5:
time: 39 us; the launch traced here: 38.8 us
  blocking collectives  29.7 us (76%)
  Pallas kernels  7.52 us (19%)
  local copies, waits for them, and re-layouts  0.9 us (2%)
  between operations  0.64 us (2%)
    all_to_all x1, blocking collectives, per_device(): lax.all_to_all(pack(phase).reshape(16, IN_ROWS, 1, LANES), 'rows', 0, 0)  16.4 us
    all_to_all x1, blocking collectives, per_device(): lax.all_to_all(result.reshape(16, OUT_ROWS, 1, LANES), 'rows', 0, 0)  13.3 us
    pallas_call x1, Pallas kernels, filter_columns(): pl.pallas_call(column_kernel, out_shape=jax.ShapeDtypeStruct((16 * OUT_RO...  6.44 us
    unnamed x2, local copies, waits for them, and re-layouts  0.9 us
    pallas_call x1, Pallas kernels, finish(): pl.pallas_call(functools.partial(finish_kernel, scale), out_shape=(jax.Sh...  0.89 us

profile of v5, /device:TPU:0, one launch (start us, length us, event | category | flops | bytes accessed | tf_op | source)
XLA Modules:
  0.0 38.8 jit_solution(6625387126786487136)
XLA Ops:
  0.6 0.0 copy-start
  0.6 0.9 %copy-done = f32[16,2048]{1,0:T(8,128)S(1)} copy-done((f32[16,2048]{1,0:T(8,128)S(1)}, f32[16,2048]{1,0:T(8,128)}, u32[]{:S(2)}) %copy-start) | copy-done | bytes 131096
  1.5 0.2 pack.1
  1.7 16.4 %all_to_all.10 = f32[16,26,1,128]{3,2,1,0:T(1,128)S(1)} all-to-all(f32[16,26,1,128]{3,2,1,0:T(1,128)S(1)} %bitcast.7), channel_id=1, replica_groups=mesh['groups'=2,'rows'=16] {'rows'}, dimensions={0} | all-to-all | bytes 425984 | tf_op jit(solution)/shard_map/all_to_all | solution.py:728
  18.2 6.4 %filter_columns.1 = f32[592,128]{1,0:T(8,128)S(1)} custom-call(f32[416,128]{1,0:T(8,128)S(1)} %bitcast.6), custom_call_target="tpu_custom_call" | custom-call | tf_op jit(solution)/shard_map/filter_columns/pallas_call | solution.py:652
  24.6 13.3 %all_to_all.11 = f32[16,37,1,128]{3,2,1,0:T(1,128)S(1)} all-to-all(f32[16,37,1,128]{3,2,1,0:T(1,128)S(1)} %bitcast.5), channel_id=1, replica_groups=mesh['groups'=2,'rows'=16] {'rows'}, dimensions={0} | all-to-all | bytes 606208 | tf_op jit(solution)/shard_map/all_to_all | solution.py:730
  37.9 0.9 %finish.1 = (f32[2,16,2048]{2,1,0:T(8,128)}, f32[3,16]{1,0:T(4,128)}) custom-call(f32[592,128]{1,0:T(8,128)S(1)} %bitcast.4), custom_call_target="tpu_custom_call" | custom-call | tf_op jit(solution)/shard_map/finish/pallas_call | solution.py:691
Async XLA Ops:
  0.6 0.9 %copy-start = (f32[16,2048]{1,0:T(8,128)S(1)}, f32[16,2048]{1,0:T(8,128)}, u32[]{:S(2)}) copy-start(f32[16,2048]{1,0:T(8,128)} %in_ref.1) | copy-start | bytes 393220

commit v6 on v5

--- a/solution.py
+++ b/solution.py
@@ -13,7 +13,7 @@
 LANES = 128
 IN_ROWS = 26
 OUT_ROWS = 37
-PITCH = 40
+PITCH = 41
 HALO = 3
 
 SIN = (9.99999996e-01, -1.66666580e-01, 8.33305053e-03, -1.98090400e-04, 2.60515161e-06)
@@ -423,7 +423,8 @@
     for k, offset in enumerate((0, 8, 16)):
         turned = stacked(offset).T
         for b in range(8):
-            turn[k * 136 + b * 17 : k * 136 + b * 17 + 16, :] = turned[b * 16 : b * 16 + 16]
+            at = k * 136 + (b % 4 * 2 + b // 4 if k == 2 else b) * 17
+            turn[at : at + 16, :] = turned[b * 16 : b * 16 + 16]
     tail = jnp.concatenate([in_ref[a * IN_ROWS + 24 : a * IN_ROWS + 26, :] for a in range(16)], axis=0)
     for q in range(4):
         for u in range(4):
@@ -432,24 +433,22 @@
     turned = turn[408:536, :].T[0:32]
     beyond = jnp.where(tile * 8 + 10 < 128, 1.0, 0.0)
     for ref, v in zip((zr, zi), cos_sin(turned)):
-        for k in range(32):
-            at = (k % 16) * PITCH + 24 + k // 16
-            ref[at : at + 1, :] = v[k : k + 1] * beyond
+        for k in range(4):
+            at = (k % 2) * 8 * PITCH + 24 + k // 2
+            ref[pl.ds(at, 8, stride=PITCH), :] = v[k * 8 : k * 8 + 8] * beyond
     for g in range(2):
         for s in range(16):
             value = cos_sin(turn[pl.ds(g * 136 + s, 8, stride=17), :])
             for ref, v in zip((zr, zi), value):
                 ref[pl.ds(s * PITCH + 4 + g, 8, stride=2), :] = v
-    edge = tile * 8 + jnp.where((sub & 3) < 2, 8 + (sub & 3), (sub & 3) - 4)
+    edge = tile * 8 + jnp.where(sub < 4, 8 + sub // 2, sub // 2 - 4)
     edge = jnp.where((edge >= 0) & (edge < 128), 1.0, 0.0)
     for s in range(16):
         value = cos_sin(turn[pl.ds(272 + s, 8, stride=17), :])
         for ref, v in zip((zr, zi), value):
             v = v * edge
-            for g in range(2):
-                for k, place in enumerate((10, 11, 0, 1)):
-                    at = s * PITCH + 2 * place + g
-                    ref[at : at + 1, :] = v[g * 4 + k : g * 4 + k + 1]
+            ref[s * PITCH + 20 : s * PITCH + 24, :] = v[0:4]
+            ref[s * PITCH : s * PITCH + 4, :] = v[4:8]
 
     def forward_columns(first, width, j):
         near = []
@@ -592,19 +591,15 @@
     for k in range(32):
         final[1][k * 19 : k * 19 + 2, :] = zero[0:2]
 
-    for step in range(ITERS):
-        first = step
-        valid = 12 - 2 * step
-        width = -(-valid // 4) * 4
+    def iteration(step, width, last):
         chunks = width // 4
-        last = step == ITERS - 1
-        run(chunks, functools.partial(forward_columns, first, width))
+        run(chunks, functools.partial(forward_columns, step, width))
 
         @block
         def _():
-            window_gains(valid, width)
+            window_gains(12 - 2 * step, width)
             turn_in(0)
-            final[2][step * 8 : step * 8 + 8, :] = residues()
+            final[2][pl.ds(step * 8, 8), :] = residues()
 
         for chunk in range(chunks):
 
@@ -618,7 +613,10 @@
                     turn_out(chunk - 1)
 
         block(lambda: turn_out(chunks - 1))
-        run(chunks, functools.partial(inverse_columns, first, width, last))
+        run(chunks, functools.partial(inverse_columns, step, width, last))
+
+    run(ITERS - 1, lambda step: iteration(step, 12, False))
+    iteration(ITERS - 1, 8, True)
 
     spill = []
     for part in range(2):
@@ -665,7 +663,7 @@
     )(data)
 
 
-def finish_kernel(scale, in_ref, field_ref, profile_ref):
+def finish_kernel(scale, in_ref, field_ref, profile_ref, rows, sent):
     lane = lax.broadcasted_iota(jnp.int32, (8, LANES), 1)
     extras = []
     sums = jnp.zeros((1, LANES), jnp.float32)
@@ -675,16 +673,19 @@
         sums = sums + in_ref[c * OUT_ROWS + 36 : c * OUT_ROWS + 37, :]
     for step in range(ITERS):
         profile_ref[step : step + 1, :] = sums[:, step * 16 : step * 16 + 16] * scale
-    for part in range(2):
-        for g in range(2):
-            offset = (part * 2 + g) * 16
-            for c in range(16):
-                at = c * OUT_ROWS + part * 16 + g * 8
-                value = in_ref[at : at + 8, :]
-                if c:
-                    spill = pltpu.roll(extras[c - 1], LANES - offset, 1) if offset else extras[c - 1]
-                    value = value + jnp.where(lane < 16, spill, 0.0)
-                field_ref[part, g * 8 : g * 8 + 8, c * LANES : (c + 1) * LANES] = value
+    copies = []
+    for k in range(4):
+        part, g = k // 2, k % 2
+        for c in range(16):
+            value = in_ref[c * OUT_ROWS + k * 8 : c * OUT_ROWS + k * 8 + 8, :]
+            if c:
+                spill = pltpu.roll(extras[c - 1], LANES - k * 16, 1) if k else extras[c - 1]
+                value = value + jnp.where(lane < 16, spill, 0.0)
+            rows[k, :, c * LANES : (c + 1) * LANES] = value
+        copies.append(pltpu.make_async_copy(rows.at[k], field_ref.at[part, pl.ds(g * 8, 8)], sent.at[k]))
+        copies[-1].start()
+    for copy in copies:
+        copy.wait()
 
 
 def finish(scale, data):
@@ -695,7 +696,8 @@
             jax.ShapeDtypeStruct((ITERS, 16), jnp.float32),
         ),
         in_specs=[pl.BlockSpec(memory_space=pltpu.VMEM)],
-        out_specs=[pl.BlockSpec(memory_space=pltpu.VMEM)] * 2,
+        out_specs=[pl.BlockSpec(memory_space=pl.ANY), pl.BlockSpec(memory_space=pltpu.VMEM)],
+        scratch_shapes=[pltpu.VMEM((4, 8, 16 * LANES), jnp.float32), pltpu.SemaphoreType.DMA((4,))],
         compiler_params=pltpu.CompilerParams(vmem_limit_bytes=8 << 20),
         name="finish",
     )(data)

time: 39 us -> 39.5 us (1.013)
  Pallas kernels: 7.52 us -> 8.03 us
    pallas_call x1, Pallas kernels: 0.89 us -> 1.44 us  [finish(): pl.pallas_call(functools.partial(finish_kernel, scale), out_shape=(jax.Sh...]
where the time goes in v6:
time: 39.5 us; the launch traced here: 39.3 us
  blocking collectives  29.7 us (75%)
  Pallas kernels  8.03 us (20%)
  local copies, waits for them, and re-layouts  0.9 us (2%)
  between operations  0.64 us (2%)
    all_to_all x1, blocking collectives, per_device(): lax.all_to_all(pack(phase).reshape(16, IN_ROWS, 1, LANES), 'rows', 0, 0)  16.4 us
    all_to_all x1, blocking collectives, per_device(): lax.all_to_all(result.reshape(16, OUT_ROWS, 1, LANES), 'rows', 0, 0)  13.3 us
    pallas_call x1, Pallas kernels, filter_columns(): pl.pallas_call(column_kernel, out_shape=jax.ShapeDtypeStruct((16 * OUT_RO...  6.41 us
    pallas_call x1, Pallas kernels, finish(): pl.pallas_call(functools.partial(finish_kernel, scale), out_shape=(jax.Sh...  1.44 us
    unnamed x2, local copies, waits for them, and re-layouts  0.9 us

profile of v6, /device:TPU:0, one launch (start us, length us, event | category | flops | bytes accessed | tf_op | source)
XLA Modules:
  0.0 39.3 jit_solution(6719492222478423700)
XLA Ops:
  0.6 0.0 copy-start
  0.6 0.9 %copy-done = f32[16,2048]{1,0:T(8,128)S(1)} copy-done((f32[16,2048]{1,0:T(8,128)S(1)}, f32[16,2048]{1,0:T(8,128)}, u32[]{:S(2)}) %copy-start) | copy-done | bytes 131096
  1.5 0.2 pack.1
  1.7 16.4 %all_to_all.10 = f32[16,26,1,128]{3,2,1,0:T(1,128)S(1)} all-to-all(f32[16,26,1,128]{3,2,1,0:T(1,128)S(1)} %bitcast.7), channel_id=1, replica_groups=mesh['groups'=2,'rows'=16] {'rows'}, dimensions={0} | all-to-all | bytes 425984 | tf_op jit(solution)/shard_map/all_to_all | solution.py:730
  18.2 6.4 %filter_columns.1 = f32[592,128]{1,0:T(8,128)S(1)} custom-call(f32[416,128]{1,0:T(8,128)S(1)} %bitcast.6), custom_call_target="tpu_custom_call" | custom-call | tf_op jit(solution)/shard_map/filter_columns/pallas_call | solution.py:650
  24.6 13.3 %all_to_all.11 = f32[16,37,1,128]{3,2,1,0:T(1,128)S(1)} all-to-all(f32[16,37,1,128]{3,2,1,0:T(1,128)S(1)} %bitcast.5), channel_id=1, replica_groups=mesh['groups'=2,'rows'=16] {'rows'}, dimensions={0} | all-to-all | bytes 606208 | tf_op jit(solution)/shard_map/all_to_all | solution.py:732
  37.8 1.4 %finish.1 = (f32[2,16,2048]{2,1,0:T(8,128)}, f32[3,16]{1,0:T(4,128)}) custom-call(f32[592,128]{1,0:T(8,128)S(1)} %bitcast.4), custom_call_target="tpu_custom_call" | custom-call | tf_op jit(solution)/shard_map/finish/pallas_call | solution.py:692
Async XLA Ops:
  0.6 0.9 %copy-start = (f32[16,2048]{1,0:T(8,128)S(1)}, f32[16,2048]{1,0:T(8,128)}, u32[]{:S(2)}) copy-start(f32[16,2048]{1,0:T(8,128)} %in_ref.1) | copy-start | bytes 393220

commit v7 on v6

--- a/solution.py
+++ b/solution.py
@@ -663,7 +663,7 @@
     )(data)
 
 
-def finish_kernel(scale, in_ref, field_ref, profile_ref, rows, sent):
+def finish_kernel(scale, in_ref, field_ref, profile_ref):
     lane = lax.broadcasted_iota(jnp.int32, (8, LANES), 1)
     extras = []
     sums = jnp.zeros((1, LANES), jnp.float32)
@@ -673,19 +673,16 @@
         sums = sums + in_ref[c * OUT_ROWS + 36 : c * OUT_ROWS + 37, :]
     for step in range(ITERS):
         profile_ref[step : step + 1, :] = sums[:, step * 16 : step * 16 + 16] * scale
-    copies = []
-    for k in range(4):
-        part, g = k // 2, k % 2
-        for c in range(16):
-            value = in_ref[c * OUT_ROWS + k * 8 : c * OUT_ROWS + k * 8 + 8, :]
-            if c:
-                spill = pltpu.roll(extras[c - 1], LANES - k * 16, 1) if k else extras[c - 1]
-                value = value + jnp.where(lane < 16, spill, 0.0)
-            rows[k, :, c * LANES : (c + 1) * LANES] = value
-        copies.append(pltpu.make_async_copy(rows.at[k], field_ref.at[part, pl.ds(g * 8, 8)], sent.at[k]))
-        copies[-1].start()
-    for copy in copies:
-        copy.wait()
+    for part in range(2):
+        for g in range(2):
+            offset = (part * 2 + g) * 16
+            for c in range(16):
+                at = c * OUT_ROWS + part * 16 + g * 8
+                value = in_ref[at : at + 8, :]
+                if c:
+                    spill = pltpu.roll(extras[c - 1], LANES - offset, 1) if offset else extras[c - 1]
+                    value = value + jnp.where(lane < 16, spill, 0.0)
+                field_ref[part, g * 8 : g * 8 + 8, c * LANES : (c + 1) * LANES] = value
 
 
 def finish(scale, data):
@@ -696,8 +693,7 @@
             jax.ShapeDtypeStruct((ITERS, 16), jnp.float32),
         ),
         in_specs=[pl.BlockSpec(memory_space=pltpu.VMEM)],
-        out_specs=[pl.BlockSpec(memory_space=pl.ANY), pl.BlockSpec(memory_space=pltpu.VMEM)],
-        scratch_shapes=[pltpu.VMEM((4, 8, 16 * LANES), jnp.float32), pltpu.SemaphoreType.DMA((4,))],
+        out_specs=[pl.BlockSpec(memory_space=pltpu.VMEM)] * 2,
         compiler_params=pltpu.CompilerParams(vmem_limit_bytes=8 << 20),
         name="finish",
     )(data)

time: 39.5 us -> 39 us (0.987)
  Pallas kernels: 8.03 us -> 7.48 us
    pallas_call x1, Pallas kernels: 1.44 us -> 0.89 us  [finish(): pl.pallas_call(functools.partial(finish_kernel, scale), out_shape=(jax.Sh...]
where the time goes in v7:
time: 39 us; the launch traced here: 38.7 us
  blocking collectives  29.7 us (76%)
  Pallas kernels  7.48 us (19%)
  local copies, waits for them, and re-layouts  0.9 us (2%)
  between operations  0.64 us (2%)
    all_to_all x1, blocking collectives, per_device(): lax.all_to_all(pack(phase).reshape(16, IN_ROWS, 1, LANES), 'rows', 0, 0)  16.4 us
    all_to_all x1, blocking collectives, per_device(): lax.all_to_all(result.reshape(16, OUT_ROWS, 1, LANES), 'rows', 0, 0)  13.3 us
    pallas_call x1, Pallas kernels, filter_columns(): pl.pallas_call(column_kernel, out_shape=jax.ShapeDtypeStruct((16 * OUT_RO...  6.41 us
    unnamed x2, local copies, waits for them, and re-layouts  0.9 us
    pallas_call x1, Pallas kernels, finish(): pl.pallas_call(functools.partial(finish_kernel, scale), out_shape=(jax.Sh...  0.89 us

profile of v7, /device:TPU:0, one launch (start us, length us, event | category | flops | bytes accessed | tf_op | source)
XLA Modules:
  0.0 38.7 jit_solution(8983952621881094939)
XLA Ops:
  0.6 0.0 copy-start
  0.6 0.9 %copy-done = f32[16,2048]{1,0:T(8,128)S(1)} copy-done((f32[16,2048]{1,0:T(8,128)S(1)}, f32[16,2048]{1,0:T(8,128)}, u32[]{:S(2)}) %copy-start) | copy-done | bytes 131096
  1.5 0.2 pack.1
  1.7 16.4 %all_to_all.10 = f32[16,26,1,128]{3,2,1,0:T(1,128)S(1)} all-to-all(f32[16,26,1,128]{3,2,1,0:T(1,128)S(1)} %bitcast.7), channel_id=1, replica_groups=mesh['groups'=2,'rows'=16] {'rows'}, dimensions={0} | all-to-all | bytes 425984 | tf_op jit(solution)/shard_map/all_to_all | solution.py:726
  18.2 6.4 %filter_columns.1 = f32[592,128]{1,0:T(8,128)S(1)} custom-call(f32[416,128]{1,0:T(8,128)S(1)} %bitcast.6), custom_call_target="tpu_custom_call" | custom-call | tf_op jit(solution)/shard_map/filter_columns/pallas_call | solution.py:650
  24.6 13.3 %all_to_all.11 = f32[16,37,1,128]{3,2,1,0:T(1,128)S(1)} all-to-all(f32[16,37,1,128]{3,2,1,0:T(1,128)S(1)} %bitcast.5), channel_id=1, replica_groups=mesh['groups'=2,'rows'=16] {'rows'}, dimensions={0} | all-to-all | bytes 606208 | tf_op jit(solution)/shard_map/all_to_all | solution.py:728
  37.8 0.9 %finish.1 = (f32[2,16,2048]{2,1,0:T(8,128)}, f32[3,16]{1,0:T(4,128)}) custom-call(f32[592,128]{1,0:T(8,128)S(1)} %bitcast.4), custom_call_target="tpu_custom_call" | custom-call | tf_op jit(solution)/shard_map/finish/pallas_call | solution.py:689
Async XLA Ops:
  0.6 0.9 %copy-start = (f32[16,2048]{1,0:T(8,128)S(1)}, f32[16,2048]{1,0:T(8,128)}, u32[]{:S(2)}) copy-start(f32[16,2048]{1,0:T(8,128)} %in_ref.1) | copy-start | bytes 393220

commit v8 on v7

--- a/solution.py
+++ b/solution.py
@@ -3,6 +3,7 @@
 
 import jax
 import jax.numpy as jnp
+import numpy as np
 from jax import lax
 from jax.experimental import pallas as pl
 from jax.experimental.pallas import tpu as pltpu
@@ -389,10 +390,24 @@
     )(phase)
 
 
-def column_kernel(in_ref, out_ref, *scratch):
+def row_matrices():
+    k = np.arange(32)
+    angle = 2 * np.pi * (k[:, None] * k[None, :] % 32) / 32
+    cos, sin = np.cos(angle), np.sin(angle)
+    weight = np.array([ramp(t) / 32 for t in range(32)])[:, None]
+    result = []
+    for matrix in (np.block([[cos, sin], [-sin, cos]]), np.block([[cos * weight, -sin * weight], [sin * weight, cos * weight]])):
+        whole = jnp.asarray(matrix, jnp.float32)
+        high = whole.astype(jnp.bfloat16)
+        low = (whole - high.astype(jnp.float32)).astype(jnp.bfloat16)
+        result.append(jnp.concatenate([high, low, high], axis=1))
+    return result
+
+
+def column_kernel(in_ref, forward_ref, inverse_ref, out_ref, *scratch):
     zr, zi, yr, yi, wr, wi, shift_r, shift_i, gain, turn = scratch[:10]
-    buffers = [scratch[10 + 6 * k : 16 + 6 * k] for k in range(2)]
-    final = scratch[22:25]
+    buffers = [scratch[10 + 8 * k : 18 + 8 * k] for k in range(2)]
+    final = scratch[26:29]
     tile = lax.axis_index("rows")
     lane = lax.broadcasted_iota(jnp.int32, (8, LANES), 1)
     sub = lax.broadcasted_iota(jnp.int32, (8, LANES), 0)
@@ -409,13 +424,12 @@
         lax.fori_loop(0, count, lambda i, c: (body(i), c)[1], 0)
 
     zero = jnp.zeros((8, LANES), jnp.float32)
-    for vr, vi, pr, pi, qr, qi in buffers:
-        for ref in (vr, vi):
-            for row in (272, 280, 288):
-                ref[row : row + 8, :] = zero
-        for ref in (qr, qi):
-            for t in range(16):
-                ref[t * 17 : t * 17 + 1, :] = zero[0:1]
+    for part in buffers:
+        for ref in part[:4]:
+            ref[256:272, :] = jnp.zeros((16, LANES), jnp.bfloat16)
+        for ref in part[6:8]:
+            ref[0:8, :] = zero
+            ref[8:16, :] = zero
 
     def stacked(offset):
         return jnp.concatenate([in_ref[a * IN_ROWS + offset : a * IN_ROWS + offset + 8, :] for a in range(16)], axis=0)
@@ -468,23 +482,26 @@
             to = pl.ds(l * 2 * width + j * 8, 8)
             yr[to, :], yi[to, :] = (even, odd)[l % 2][l // 2]
 
+    def split(value):
+        high = value.astype(jnp.bfloat16)
+        return high, (value - high.astype(jnp.float32)).astype(jnp.bfloat16)
+
     def turn_in(chunk):
-        vr, vi = buffers[chunk % 2][:2]
-        for source, ref in ((yr, vr), (yi, vi)):
+        for part, source in enumerate((yr, yi)):
+            halves = []
             for g in range(2):
                 parts = [source[pl.ds(chunk * 256 + i * 16 + g, 8, stride=2), :] for i in range(16)]
-                turned = jnp.concatenate(parts, axis=0).T
-                for a in range(16):
-                    ref[a * 17 + g * 8 : a * 17 + g * 8 + 8, :] = turned[a * 8 : a * 8 + 8]
+                halves.append(jnp.concatenate(parts, axis=0).T)
+            high, low = buffers[chunk % 2][part], buffers[chunk % 2][2 + part]
+            for a in range(16):
+                value = jnp.concatenate([v[a * 8 : a * 8 + 8] for v in halves], axis=0)
+                high[a * 16 : a * 16 + 16, :], low[a * 16 : a * 16 + 16, :] = split(value)
 
     def turn_out(chunk):
-        pr, pi, qr, qi = buffers[chunk % 2][2:]
+        pr, pi, qr, qi = buffers[chunk % 2][4:]
         for p, q, target in ((pr, qr, wr), (pi, qi, wi)):
             for g in range(2):
-                parts = []
-                for a in range(16):
-                    at = pl.ds(g * 136 + a, 8, stride=17)
-                    parts.append(p[at, :] + q[at, :])
+                parts = [p[a * 16 + g * 8 : a * 16 + g * 8 + 8, :] + q[a * 16 + g * 8 : a * 16 + g * 8 + 8, :] for a in range(16)]
                 turned = jnp.concatenate(parts, axis=0).T
                 for i in range(16):
                     target[pl.ds(chunk * 256 + i * 16 + g, 8, stride=2), :] = turned[i * 8 : i * 8 + 8]
@@ -536,33 +553,24 @@
             here, down = following, following_down
         return total
 
-    def windows(chunk, half):
-        vr, vi, pr, pi, qr, qi = buffers[chunk % 2]
-        scale = gain[chunk * 16 + half * 8 : chunk * 16 + half * 8 + 8, :]
-        sums = []
-        differences = []
-        for t in range(16):
-            at = pl.ds(half * 136 + t, 8, stride=17)
-            after = pl.ds(half * 136 + 17 + t, 8, stride=17)
-            near = (vr[at, :], vi[at, :])
-            far = (vr[after, :], vi[after, :])
-            sums.append(plus(near, far))
-            differences.append(minus(near, far))
-        back = []
-        for spectrum in (lambda: fft(sums, -1), lambda: odd_outputs(differences)):
-            filtered = []
-            for re, im in spectrum():
-                factor = lax.rsqrt(lax.rsqrt((re * re + im * im) * scale))
-                filtered.append((re * factor, im * factor))
-            back.append(filtered)
-        back = fft(back[0], 1), join(fft(back[1][0::2], 1), fft(back[1][1::2], 1), 32, 1)
-        for t in range(16):
-            upper = plus(back[0][t], back[1][t])
-            lower = minus(back[0][t], back[1][t])
-            at = pl.ds(t * 17 + half * 8, 8)
-            pr[at, :], pi[at, :] = (v * (ramp(t) / 32) for v in upper)
-            at = pl.ds(t * 17 + half * 8 + 1, 8)
-            qr[at, :], qi[at, :] = (v * (ramp(t + 16) / 32) for v in lower)
+    def windows(chunk, pair):
+        hr, hi, lr, li, pr, pi, qr, qi = buffers[chunk % 2]
+        data = []
+        scale = []
+        for a in (2 * pair, 2 * pair + 1):
+            rows = slice(a * 16, a * 16 + 32)
+            data.append(jnp.concatenate([hr[rows, :], hi[rows, :], hr[rows, :], hi[rows, :], lr[rows, :], li[rows, :]], axis=0))
+            scale.append(jnp.broadcast_to(gain[chunk * 16 + a : chunk * 16 + a + 1, :], (32, LANES)))
+        spectrum = jnp.dot(forward_ref[...], jnp.concatenate(data, axis=1), preferred_element_type=jnp.float32)
+        re, im = spectrum[0:32], spectrum[32:64]
+        factor = lax.rsqrt(lax.rsqrt((re * re + im * im) * jnp.concatenate(scale, axis=1)))
+        high, low = split(jnp.concatenate([re * factor, im * factor], axis=0))
+        back = jnp.dot(inverse_ref[...], jnp.concatenate([high, high, low], axis=0), preferred_element_type=jnp.float32)
+        for k in range(2):
+            at = (2 * pair + k) * 16
+            part = back[:, k * LANES : (k + 1) * LANES]
+            pr[at : at + 16, :], qr[at + 16 : at + 32, :] = part[0:16], part[16:32]
+            pi[at : at + 16, :], qi[at + 16 : at + 32, :] = part[32:48], part[48:64]
 
     def inverse_columns(first, width, last, j):
         here = inside(first + 4 * j)
@@ -607,8 +615,8 @@
             def _():
                 if chunk + 1 < chunks:
                     turn_in(chunk + 1)
-                windows(chunk, 0)
-                windows(chunk, 1)
+                for pair in range(8):
+                    windows(chunk, pair)
                 if chunk:
                     turn_out(chunk - 1)
 
@@ -650,17 +658,17 @@
     return pl.pallas_call(
         column_kernel,
         out_shape=jax.ShapeDtypeStruct((16 * OUT_ROWS, LANES), jnp.float32),
-        in_specs=[pl.BlockSpec(memory_space=pltpu.VMEM)],
+        in_specs=[pl.BlockSpec(memory_space=pltpu.VMEM)] * 3,
         out_specs=pl.BlockSpec(memory_space=pltpu.VMEM),
         scratch_shapes=[rows(16 * PITCH)] * 2
         + [rows(776)] * 4
         + [rows(520)] * 2
         + [rows(80), rows(544)]
-        + ([rows(296)] * 2 + [rows(280)] * 4) * 2
+        + ([pltpu.VMEM((272, LANES), jnp.bfloat16)] * 4 + [rows(272)] * 4) * 2
         + [rows(624), rows(624), rows(ITERS * 8)],
         compiler_params=pltpu.CompilerParams(vmem_limit_bytes=16 << 20),
         name="filter_columns",
-    )(data)
+    )(data, *row_matrices())
 
 
 def finish_kernel(scale, in_ref, field_ref, profile_ref):

time: 39 us -> 38.2 us (0.979)
  Pallas kernels: 7.48 us -> 6.63 us
    pallas_call x1, Pallas kernels: 6.41 us -> 5.55 us  [filter_columns(): pl.pallas_call(column_kernel, out_shape=jax.ShapeDtypeStruct((16 * OUT_RO...]
    unnamed x2 -> x6, local copies, waits for them, and re-layouts: 0.9 us -> 0.91 us
where the time goes in v8:
time: 38.2 us; the launch traced here: 37.9 us
  blocking collectives  29.7 us (78%)
  Pallas kernels  6.63 us (17%)
  local copies, waits for them, and re-layouts  0.91 us (2%)
  between operations  0.66 us (2%)
    all_to_all x1, blocking collectives, per_device(): lax.all_to_all(pack(phase).reshape(16, IN_ROWS, 1, LANES), 'rows', 0, 0)  16.4 us
    all_to_all x1, blocking collectives, per_device(): lax.all_to_all(result.reshape(16, OUT_ROWS, 1, LANES), 'rows', 0, 0)  13.3 us
    pallas_call x1, Pallas kernels, filter_columns(): pl.pallas_call(column_kernel, out_shape=jax.ShapeDtypeStruct((16 * OUT_RO...  5.55 us
    unnamed x6, local copies, waits for them, and re-layouts  0.91 us
    pallas_call x1, Pallas kernels, finish(): pl.pallas_call(functools.partial(finish_kernel, scale), out_shape=(jax.Sh...  0.89 us

profile of v8, /device:TPU:0, one launch (start us, length us, event | category | flops | bytes accessed | tf_op | source)
XLA Modules:
  0.0 37.9 jit_solution(6772513844501369863)
XLA Ops:
  0.6 0.0 copy-start
  0.6 0.9 %copy-done = f32[16,2048]{1,0:T(8,128)S(1)} copy-done((f32[16,2048]{1,0:T(8,128)S(1)}, f32[16,2048]{1,0:T(8,128)}, u32[]{:S(2)}) %copy-start) | copy-done | bytes 131096
  1.5 0.2 pack.1
  1.7 0.0 copy-start.1
  1.7 0.0 copy-start.2
  1.7 16.4 %all_to_all.10 = f32[16,26,1,128]{3,2,1,0:T(1,128)S(1)} all-to-all(f32[16,26,1,128]{3,2,1,0:T(1,128)S(1)} %bitcast.7), channel_id=1, replica_groups=mesh['groups'=2,'rows'=16] {'rows'}, dimensions={0} | all-to-all | bytes 425984 | tf_op jit(solution)/shard_map/all_to_all | solution.py:734
  18.2 0.0 copy-done.1
  18.2 0.0 copy-done.2
  18.2 5.6 %filter_columns.1 = f32[592,128]{1,0:T(8,128)S(1)} custom-call(f32[416,128]{1,0:T(8,128)S(1)} %bitcast.6, bf16[64,192]{1,0:T(8,128)(2,1)S(1)} %copy-done.2, bf16[64,192]{1,0:T(8,128)(2,1)S(1)} %copy-done.1), custom_call_target="tpu_custom_call" | custom-call | tf_op jit(solution)/shard_map/filter_columns/pallas_call | solution.py:658
  23.7 13.3 %all_to_all.11 = f32[16,37,1,128]{3,2,1,0:T(1,128)S(1)} all-to-all(f32[16,37,1,128]{3,2,1,0:T(1,128)S(1)} %bitcast.4), channel_id=1, replica_groups=mesh['groups'=2,'rows'=16] {'rows'}, dimensions={0} | all-to-all | bytes 606208 | tf_op jit(solution)/shard_map/all_to_all | solution.py:736
  37.0 0.9 %finish.1 = (f32[2,16,2048]{2,1,0:T(8,128)}, f32[3,16]{1,0:T(4,128)}) custom-call(f32[592,128]{1,0:T(8,128)S(1)} %bitcast.5), custom_call_target="tpu_custom_call" | custom-call | tf_op jit(solution)/shard_map/finish/pallas_call | solution.py:697
Async XLA Ops:
  0.6 0.9 %copy-start = (f32[16,2048]{1,0:T(8,128)S(1)}, f32[16,2048]{1,0:T(8,128)}, u32[]{:S(2)}) copy-start(f32[16,2048]{1,0:T(8,128)} %in_ref.1) | copy-start | bytes 393220
  1.7 16.5 %copy-start.1 = (bf16[64,192]{1,0:T(8,128)(2,1)S(1)}, bf16[64,192]{1,0:T(8,128)(2,1)}, u32[]{:S(2)}) copy-start(bf16[64,192]{1,0:T(8,128)(2,1)} %constant.16.inverse_ref) | copy-start | bytes 73732
  1.7 16.5 %copy-start.2 = (bf16[64,192]{1,0:T(8,128)(2,1)S(1)}, bf16[64,192]{1,0:T(8,128)(2,1)}, u32[]{:S(2)}) copy-start(bf16[64,192]{1,0:T(8,128)(2,1)} %constant.11.forward_ref) | copy-start | bytes 73732

commit v9 on v8

--- a/solution.py
+++ b/solution.py
@@ -479,7 +479,7 @@
         even = fft([plus(a, b) for a, b in zip(near, far)], -1)
         odd = odd_outputs([minus(a, b) for a, b in zip(near, far)])
         for l in range(32):
-            to = pl.ds(l * 2 * width + j * 8, 8)
+            to = pl.ds(j * 256 + l * 8, 8)
             yr[to, :], yi[to, :] = (even, odd)[l % 2][l // 2]
 
     def split(value):
@@ -517,7 +517,7 @@
         exact = dict(precision=lax.Precision.HIGHEST, preferred_element_type=jnp.float32)
         mean = lax.dot_general(pick, power, (((1,), (1,)), ((), ())), **exact)
         column = lax.broadcasted_iota(jnp.int32, (count, 32 * width), 1)
-        column = column - width * ((column.astype(jnp.float32) + 0.5) * (1.0 / width)).astype(jnp.int32)
+        column = column // 128 * 4 + column % 4
         spread = jnp.where(column == lax.broadcasted_iota(jnp.int32, (count, 32 * width), 0) // 2, 1.0, 0.0)
         mean = lax.dot_general(mean, spread, (((1,), (0,)), ((), ())), **exact)
         for c in range(width // 4):
@@ -577,7 +577,7 @@
         both = here * inside(first + 4 * j + 1)
         values = []
         for l in range(32):
-            at = pl.ds(l * 2 * width + 8 * j, 8)
+            at = pl.ds(j * 256 + l * 8, 8)
             values.append((wr[at, :], wi[at, :]))
         even = fft(values[0::2], 1)
         odd = join(fft(values[1::4], 1), fft(values[3::4], 1), 32, 1)
@@ -601,10 +601,10 @@
 
     def iteration(step, width, last):
         chunks = width // 4
-        run(chunks, functools.partial(forward_columns, step, width))
-
         @block
         def _():
+            for j in range(chunks):
+                forward_columns(step, width, j)
             window_gains(12 - 2 * step, width)
             turn_in(0)
             final[2][pl.ds(step * 8, 8), :] = residues()
@@ -620,8 +620,11 @@
                 if chunk:
                     turn_out(chunk - 1)
 
-        block(lambda: turn_out(chunks - 1))
-        run(chunks, functools.partial(inverse_columns, step, width, last))
+        @block
+        def _():
+            turn_out(chunks - 1)
+            for j in range(chunks):
+                inverse_columns(step, width, last, j)
 
     run(ITERS - 1, lambda step: iteration(step, 12, False))
     iteration(ITERS - 1, 8, True)

time: 38.2 us -> 37.4 us (0.979)
  Pallas kernels: 6.63 us -> 5.9 us
    pallas_call x1, Pallas kernels: 5.55 us -> 4.82 us  [filter_columns(): pl.pallas_call(column_kernel, out_shape=jax.ShapeDtypeStruct((16 * OUT_RO...]
where the time goes in v9:
time: 37.4 us; the launch traced here: 37.2 us
  blocking collectives  29.7 us (79%)
  Pallas kernels  5.9 us (16%)
  local copies, waits for them, and re-layouts  0.91 us (2%)
  between operations  0.66 us (2%)
    all_to_all x1, blocking collectives, per_device(): lax.all_to_all(pack(phase).reshape(16, IN_ROWS, 1, LANES), 'rows', 0, 0)  16.4 us
    all_to_all x1, blocking collectives, per_device(): lax.all_to_all(result.reshape(16, OUT_ROWS, 1, LANES), 'rows', 0, 0)  13.3 us
    pallas_call x1, Pallas kernels, filter_columns(): pl.pallas_call(column_kernel, out_shape=jax.ShapeDtypeStruct((16 * OUT_RO...  4.82 us
    unnamed x6, local copies, waits for them, and re-layouts  0.91 us
    pallas_call x1, Pallas kernels, finish(): pl.pallas_call(functools.partial(finish_kernel, scale), out_shape=(jax.Sh...  0.89 us

profile of v9, /device:TPU:0, one launch (start us, length us, event | category | flops | bytes accessed | tf_op | source)
XLA Modules:
  0.0 37.2 jit_solution(14458874914253592562)
XLA Ops:
  0.6 0.0 copy-start
  0.6 0.9 %copy-done = f32[16,2048]{1,0:T(8,128)S(1)} copy-done((f32[16,2048]{1,0:T(8,128)S(1)}, f32[16,2048]{1,0:T(8,128)}, u32[]{:S(2)}) %copy-start) | copy-done | bytes 131096
  1.5 0.2 pack.1
  1.7 0.0 copy-start.1
  1.7 0.0 copy-start.2
  1.7 16.4 %all_to_all.10 = f32[16,26,1,128]{3,2,1,0:T(1,128)S(1)} all-to-all(f32[16,26,1,128]{3,2,1,0:T(1,128)S(1)} %bitcast.7), channel_id=1, replica_groups=mesh['groups'=2,'rows'=16] {'rows'}, dimensions={0} | all-to-all | bytes 425984 | tf_op jit(solution)/shard_map/all_to_all | solution.py:737
  18.2 0.0 copy-done.1
  18.2 0.0 copy-done.2
  18.2 4.8 %filter_columns.1 = f32[592,128]{1,0:T(8,128)S(1)} custom-call(f32[416,128]{1,0:T(8,128)S(1)} %bitcast.6, bf16[64,192]{1,0:T(8,128)(2,1)S(1)} %copy-done.2, bf16[64,192]{1,0:T(8,128)(2,1)S(1)} %copy-done.1), custom_call_target="tpu_custom_call" | custom-call | tf_op jit(solution)/shard_map/filter_columns/pallas_call | solution.py:661
  23.0 13.3 %all_to_all.11 = f32[16,37,1,128]{3,2,1,0:T(1,128)S(1)} all-to-all(f32[16,37,1,128]{3,2,1,0:T(1,128)S(1)} %bitcast.4), channel_id=1, replica_groups=mesh['groups'=2,'rows'=16] {'rows'}, dimensions={0} | all-to-all | bytes 606208 | tf_op jit(solution)/shard_map/all_to_all | solution.py:739
  36.3 0.9 %finish.1 = (f32[2,16,2048]{2,1,0:T(8,128)}, f32[3,16]{1,0:T(4,128)}) custom-call(f32[592,128]{1,0:T(8,128)S(1)} %bitcast.5), custom_call_target="tpu_custom_call" | custom-call | tf_op jit(solution)/shard_map/finish/pallas_call | solution.py:700
Async XLA Ops:
  0.6 0.9 %copy-start = (f32[16,2048]{1,0:T(8,128)S(1)}, f32[16,2048]{1,0:T(8,128)}, u32[]{:S(2)}) copy-start(f32[16,2048]{1,0:T(8,128)} %in_ref.1) | copy-start | bytes 393220
  1.7 16.5 %copy-start.1 = (bf16[64,192]{1,0:T(8,128)(2,1)S(1)}, bf16[64,192]{1,0:T(8,128)(2,1)}, u32[]{:S(2)}) copy-start(bf16[64,192]{1,0:T(8,128)(2,1)} %constant.16.inverse_ref) | copy-start | bytes 73732
  1.7 16.5 %copy-start.2 = (bf16[64,192]{1,0:T(8,128)(2,1)S(1)}, bf16[64,192]{1,0:T(8,128)(2,1)}, u32[]{:S(2)}) copy-start(bf16[64,192]{1,0:T(8,128)(2,1)} %constant.11.forward_ref) | copy-start | bytes 73732

commit v10 on v9

--- a/solution.py
+++ b/solution.py
@@ -674,7 +674,7 @@
     )(data, *row_matrices())
 
 
-def finish_kernel(scale, in_ref, field_ref, profile_ref):
+def finish_kernel(scale, in_ref, field_ref, profile_hbm, rows, profile_ref, sent):
     lane = lax.broadcasted_iota(jnp.int32, (8, LANES), 1)
     extras = []
     sums = jnp.zeros((1, LANES), jnp.float32)
@@ -684,16 +684,20 @@
         sums = sums + in_ref[c * OUT_ROWS + 36 : c * OUT_ROWS + 37, :]
     for step in range(ITERS):
         profile_ref[step : step + 1, :] = sums[:, step * 16 : step * 16 + 16] * scale
-    for part in range(2):
-        for g in range(2):
-            offset = (part * 2 + g) * 16
-            for c in range(16):
-                at = c * OUT_ROWS + part * 16 + g * 8
-                value = in_ref[at : at + 8, :]
-                if c:
-                    spill = pltpu.roll(extras[c - 1], LANES - offset, 1) if offset else extras[c - 1]
-                    value = value + jnp.where(lane < 16, spill, 0.0)
-                field_ref[part, g * 8 : g * 8 + 8, c * LANES : (c + 1) * LANES] = value
+    copies = [pltpu.make_async_copy(profile_ref, profile_hbm, sent.at[4])]
+    copies[0].start()
+    for k in range(4):
+        part, g = k // 2, k % 2
+        for c in range(16):
+            value = in_ref[c * OUT_ROWS + k * 8 : c * OUT_ROWS + k * 8 + 8, :]
+            if c:
+                spill = pltpu.roll(extras[c - 1], LANES - k * 16, 1) if k else extras[c - 1]
+                value = value + jnp.where(lane < 16, spill, 0.0)
+            rows[k, :, c * LANES : (c + 1) * LANES] = value
+        copies.append(pltpu.make_async_copy(rows.at[k], field_ref.at[part, pl.ds(g * 8, 8)], sent.at[k]))
+        copies[-1].start()
+    for copy in copies:
+        copy.wait()
 
 
 def finish(scale, data):
@@ -704,7 +708,8 @@
             jax.ShapeDtypeStruct((ITERS, 16), jnp.float32),
         ),
         in_specs=[pl.BlockSpec(memory_space=pltpu.VMEM)],
-        out_specs=[pl.BlockSpec(memory_space=pltpu.VMEM)] * 2,
+        out_specs=[pl.BlockSpec(memory_space=pl.ANY)] * 2,
+        scratch_shapes=[pltpu.VMEM((4, 8, 16 * LANES), jnp.float32), pltpu.VMEM((ITERS, 16), jnp.float32), pltpu.SemaphoreType.DMA((5,))],
         compiler_params=pltpu.CompilerParams(vmem_limit_bytes=8 << 20),
         name="finish",
     )(data)

time: 37.4 us -> 37.4 us (level)
  no operation moved by 1% of the time
where the time goes in v10:
time: 37.4 us; the launch traced here: 37.2 us
  blocking collectives  29.7 us (79%)
  Pallas kernels  5.88 us (16%)
  local copies, waits for them, and re-layouts  0.91 us (2%)
  between operations  0.66 us (2%)
    all_to_all x1, blocking collectives, per_device(): lax.all_to_all(pack(phase).reshape(16, IN_ROWS, 1, LANES), 'rows', 0, 0)  16.4 us
    all_to_all x1, blocking collectives, per_device(): lax.all_to_all(result.reshape(16, OUT_ROWS, 1, LANES), 'rows', 0, 0)  13.3 us
    pallas_call x1, Pallas kernels, filter_columns(): pl.pallas_call(column_kernel, out_shape=jax.ShapeDtypeStruct((16 * OUT_RO...  4.82 us
    unnamed x6, local copies, waits for them, and re-layouts  0.91 us
    pallas_call x1, Pallas kernels, finish(): pl.pallas_call(functools.partial(finish_kernel, scale), out_shape=(jax.Sh...  0.87 us

profile of v10, /device:TPU:0, one launch (start us, length us, event | category | flops | bytes accessed | tf_op | source)
XLA Modules:
  0.0 37.2 jit_solution(6007721409119458047)
XLA Ops:
  0.6 0.0 copy-start
  0.6 0.9 %copy-done = f32[16,2048]{1,0:T(8,128)S(1)} copy-done((f32[16,2048]{1,0:T(8,128)S(1)}, f32[16,2048]{1,0:T(8,128)}, u32[]{:S(2)}) %copy-start) | copy-done | bytes 131096
  1.5 0.2 pack.1
  1.7 0.0 copy-start.1
  1.7 0.0 copy-start.2
  1.7 16.4 %all_to_all.10 = f32[16,26,1,128]{3,2,1,0:T(1,128)S(1)} all-to-all(f32[16,26,1,128]{3,2,1,0:T(1,128)S(1)} %bitcast.7), channel_id=1, replica_groups=mesh['groups'=2,'rows'=16] {'rows'}, dimensions={0} | all-to-all | bytes 425984 | tf_op jit(solution)/shard_map/all_to_all | solution.py:742
  18.2 0.0 copy-done.1
  18.2 0.0 copy-done.2
  18.2 4.8 %filter_columns.1 = f32[592,128]{1,0:T(8,128)S(1)} custom-call(f32[416,128]{1,0:T(8,128)S(1)} %bitcast.6, bf16[64,192]{1,0:T(8,128)(2,1)S(1)} %copy-done.2, bf16[64,192]{1,0:T(8,128)(2,1)S(1)} %copy-done.1), custom_call_target="tpu_custom_call" | custom-call | tf_op jit(solution)/shard_map/filter_columns/pallas_call | solution.py:661
  23.0 13.3 %all_to_all.11 = f32[16,37,1,128]{3,2,1,0:T(1,128)S(1)} all-to-all(f32[16,37,1,128]{3,2,1,0:T(1,128)S(1)} %bitcast.4), channel_id=1, replica_groups=mesh['groups'=2,'rows'=16] {'rows'}, dimensions={0} | all-to-all | bytes 606208 | tf_op jit(solution)/shard_map/all_to_all | solution.py:744
  36.3 0.9 %finish.1 = (f32[2,16,2048]{2,1,0:T(8,128)}, f32[3,16]{1,0:T(4,128)}) custom-call(f32[592,128]{1,0:T(8,128)S(1)} %bitcast.5), custom_call_target="tpu_custom_call" | custom-call | tf_op jit(solution)/shard_map/finish/pallas_call | solution.py:704
Async XLA Ops:
  0.6 0.9 %copy-start = (f32[16,2048]{1,0:T(8,128)S(1)}, f32[16,2048]{1,0:T(8,128)}, u32[]{:S(2)}) copy-start(f32[16,2048]{1,0:T(8,128)} %in_ref.1) | copy-start | bytes 393220
  1.7 16.5 %copy-start.1 = (bf16[64,192]{1,0:T(8,128)(2,1)S(1)}, bf16[64,192]{1,0:T(8,128)(2,1)}, u32[]{:S(2)}) copy-start(bf16[64,192]{1,0:T(8,128)(2,1)} %constant.16.inverse_ref) | copy-start | bytes 73732
  1.7 16.5 %copy-start.2 = (bf16[64,192]{1,0:T(8,128)(2,1)S(1)}, bf16[64,192]{1,0:T(8,128)(2,1)}, u32[]{:S(2)}) copy-start(bf16[64,192]{1,0:T(8,128)(2,1)} %constant.11.forward_ref) | copy-start | bytes 73732
